TPU v7x, 32 devices: a whole 2x2x4 slice. The times are simulated.
32 devices in a mesh: gx: 8 (over z, core), gy: 4 (over y, x).
Axes of the slice: x: 2, y: 2, z: 4, core: 2. Of those that a mesh axis runs over, the one named last changes fastest.
Arguments:
- potential: float32 [32, 64, 256], P('gx', 'gy'), may hold values from -0.2 to 1.2
- recovery: float32 [32, 64, 256], P('gx', 'gy'), may hold values from 0 to 1.5
- fiber_angles: float32 [2, 32, 64, 256], P(None, 'gx', 'gy'), may hold values from -3.140625 to 3.140625
- deform: float32 [9, 8192], P(None, ('gx', 'gy')), may hold values from -0.15 to 1.25, as said below
- elem_slot: int32 [8, 16, 64], P('gx', 'gy'), may hold values from 0 to 8191, as said below
Outputs:
- potential_next: float32 [32, 64, 256], P('gx', 'gy')
- recovery_next: float32 [32, 64, 256], P('gx', 'gy')
Inputs may be any that keep to these rules, and one draw needn't show every extreme that they name: `elem_slot`: entries are distinct. Slot s lies on device s / 256 (rounded down) of gx+gy. The elements of one device's block along gx and gy lie in the slots of the devices with the same index along gx, exactly 64 of them in each. `deform`: components 0, 4 and 8 (the diagonal of F) lie in 0.8 to 1.25, the other six in -0.15 to 0.15.
All inputs are finite; a program needn't handle non-finite values.
Results may differ from a plain program's by a relative error of at most 0.0003.
Values sent between devices are 32-bit elements; how exact they have to be, the bound alone decides.
A program may use at most 64 MiB of HBM per device.

v0:
```python
import functools

import jax
import jax.numpy as jnp
from jax import lax
from jax.experimental import pallas as pl
from jax.experimental.pallas import tpu as pltpu
from jax.sharding import PartitionSpec as P

MESH = pl.DeviceIdType.MESH
RATIO = 4
LANES = 128
VMEM_LIMIT = 16 * 1024 * 1024
TOP = 8

SIDES = tuple((dx, dy) for dx in (-1, 0, 1) for dy in (-1, 0, 1) if (dx, dy) != (0, 0))


def split_two(values):
    high = values.astype(jnp.bfloat16)
    low = (values - high.astype(jnp.float32)).astype(jnp.bfloat16)
    return high, low


def dot_two(values, weights):
    high, low = split_two(values)
    return jnp.dot(high, weights, preferred_element_type=jnp.float32) + jnp.dot(
        low, weights, preferred_element_type=jnp.float32
    )


def sine_cosine(angle):
    turn = jnp.floor(angle * 0.6366197723675814 + 0.5)
    rest = angle - turn * 1.5703125
    rest = rest - turn * 4.8375129699707031e-4
    rest = rest - turn * 7.549789948768648e-8
    square = rest * rest
    sine = rest + rest * square * (
        -1.6666654611e-1 + square * (8.3321608736e-3 + square * -1.9515295891e-4)
    )
    cosine = (
        1.0
        - 0.5 * square
        + square
        * square
        * (4.166664568298827e-2 + square * (-1.388731625493765e-3 + square * 2.443315711809948e-5))
    )
    size = jnp.abs(turn)
    odd = size == 1.0
    sine_part = jnp.where(odd, cosine * turn, sine)
    cosine_part = jnp.where(odd, sine * -turn, cosine)
    flip = jnp.where(size == 2.0, -1.0, 1.0)
    return sine_part * flip, cosine_part * flip


def fiber_of(azimuth, elevation):
    sin_u, cos_u = sine_cosine(azimuth)
    sin_e, cos_e = sine_cosine(elevation)
    return cos_u * cos_e, sin_u * cos_e, sin_e


def tensor_of(entries, fiber):
    def element(i, j):
        return entries[3 * (i % 3) + j % 3]

    adjugate = [
        [
            element(j + 1, i + 1) * element(j + 2, i + 2)
            - element(j + 1, i + 2) * element(j + 2, i + 1)
            for j in range(3)
        ]
        for i in range(3)
    ]
    determinant = (
        element(0, 0) * adjugate[0][0]
        + element(0, 1) * adjugate[1][0]
        + element(0, 2) * adjugate[2][0]
    )
    inverse = 1.0 / determinant
    square = inverse * inverse
    cross = 0.3 * square
    along = 0.7 * square
    pulled = [
        adjugate[i][0] * fiber[0] + adjugate[i][1] * fiber[1] + adjugate[i][2] * fiber[2]
        for i in range(3)
    ]
    scaled = [along * pulled[i] for i in range(3)]
    conduct = []
    for i, j in ((0, 0), (1, 1), (2, 2), (0, 1), (0, 2), (1, 2)):
        metric = (
            adjugate[i][0] * adjugate[j][0]
            + adjugate[i][1] * adjugate[j][1]
            + adjugate[i][2] * adjugate[j][2]
        )
        conduct.append(cross * metric + scaled[i] * pulled[j])
    return conduct


def stretch_of(entries, fiber):
    parts = [
        entries[3 * i] * fiber[0] + entries[3 * i + 1] * fiber[1] + entries[3 * i + 2] * fiber[2]
        for i in range(3)
    ]
    return jnp.sqrt(parts[0] * parts[0] + parts[1] * parts[1] + parts[2] * parts[2])


def exchange(
    across,
    down,
    sizes,
    potential,
    recovery,
    angles,
    deform,
    slots,
    cells,
    rest_in,
    held,
    near_slots,
    fibers,
    spread_y,
    spread_z,
    send_sem,
    deform_sem,
    near_sem,
    local_sem,
):
    bx, by, nz, ex, ey, ez, parts, count = sizes
    blocks = count // LANES
    gx, gy = lax.axis_index("gx"), lax.axis_index("gy")
    first_x, last_x = gx == 0, gx == across - 1
    first_y, last_y = gy == 0, gy == down - 1

    def exists(dx, dy):
        checks = []
        if dx:
            checks.append(jnp.logical_not(first_x if dx < 0 else last_x))
        if dy:
            checks.append(jnp.logical_not(first_y if dy < 0 else last_y))
        return checks[0] if len(checks) == 1 else jnp.logical_and(*checks)

    barrier = pltpu.get_barrier_semaphore()

    def row_targets(dx):
        for step in range(0 if dx else 1, down):
            yield step, lax.rem(gy + step, down)

    def greet(dx):
        for _, target in row_targets(dx):
            pl.semaphore_signal(barrier, inc=1, device_id=(gx + dx, target), device_id_type=MESH)

    pl.when(exists(-1, 0))(lambda: greet(-1))
    pl.when(exists(1, 0))(lambda: greet(1))
    greet(0)

    packed = held.at[1, gy]
    local = []

    def fetch(source, target):
        copy = pltpu.make_async_copy(source, target, local_sem.at[len(local)])
        copy.start()
        local.append(copy)

    for b in range(blocks):
        columns = pl.ds(b * LANES, LANES)
        fetch(deform.at[pl.ds(0, 8), columns], packed.at[pl.ds(8 * b, 8)])
        fetch(deform.at[pl.ds(8, 1), columns], packed.at[pl.ds(8 * blocks + b, 1)])
    fetch(slots, near_slots.at[1, 1])
    inside = pl.ds(TOP, by)
    fetch(potential, cells.at[0, pl.ds(1, bx), inside])
    fetch(angles, cells.at[pl.ds(1, 2), pl.ds(1, bx), inside])
    fetch(recovery, rest_in)
    for copy in local:
        copy.wait()

    rows_here = 1 + jnp.where(first_x, 0, 1) + jnp.where(last_x, 0, 1)
    pl.semaphore_wait(barrier, rows_here * down - 1)

    def deform_copy(dx, step, target):
        index = (1 - dx) * down + step
        rows = pl.ds(0, 9 * blocks)
        return pltpu.make_async_remote_copy(
            src_ref=held.at[1, gy, rows],
            dst_ref=held.at[1 - dx, gy, rows],
            send_sem=send_sem.at[index],
            recv_sem=deform_sem.at[index],
            device_id=(gx + dx, target),
            device_id_type=MESH,
        )

    def near_copies(dx, dy):
        place = (1 - dx) * 3 + (1 - dy)
        base = 3 * down + 2 * place
        x_source = pl.ds(1, bx) if dx == 0 else pl.ds(1 if dx < 0 else bx, 1)
        x_target = pl.ds(1, bx) if dx == 0 else pl.ds(bx + 1 if dx < 0 else 0, 1)
        y_source = inside if dy == 0 else pl.ds(TOP if dy < 0 else TOP + by - 1, 1)
        y_target = inside if dy == 0 else pl.ds(TOP + by if dy < 0 else TOP - 1, 1)
        fields = pl.ds(0, 1 if dx and dy else 3)
        pairs = [
            (near_slots.at[1, 1], near_slots.at[1 - dx, 1 - dy]),
            (cells.at[fields, x_source, y_source], cells.at[fields, x_target, y_target]),
        ]
        return [
            pltpu.make_async_remote_copy(
                src_ref=source,
                dst_ref=target,
                send_sem=send_sem.at[base + number],
                recv_sem=near_sem.at[2 * place + number],
                device_id=(gx + dx, gy + dy),
                device_id_type=MESH,
            )
            for number, (source, target) in enumerate(pairs)
        ]

    def over_row(dx, act):
        for step, target in row_targets(dx):
            act(deform_copy(dx, step, target))

    def over_near(dx, dy, act):
        for copy in near_copies(dx, dy):
            act(copy)

    def everything(act, way=1):
        def side(dx, dy):
            pl.when(exists(way * dx, way * dy))(lambda: over_near(dx, dy, act))

        for dx in (-1, 1, 0):
            if dx:
                pl.when(exists(way * dx, 0))(lambda dx=dx: over_row(dx, act))
            else:
                over_row(0, act)
        for dx, dy in SIDES:
            side(dx, dy)

    everything(lambda copy: copy.start())

    width = (ey + 2) * ez
    tall = by + 8
    row = lax.broadcasted_iota(jnp.int32, (tall, width), 0)
    lane = lax.broadcasted_iota(jnp.int32, (tall, width), 1)
    cell = jnp.where(row < by, row, jnp.where(row < by + bx, -1, by))
    spot = (cell.astype(jnp.float32) + 0.5) * (1.0 / RATIO) - 0.5
    spread_y[...] = jnp.maximum(
        1.0 - jnp.abs(spot - ((lane // ez) - 1).astype(jnp.float32)), 0.0
    )
    row = lax.broadcasted_iota(jnp.int32, (width, nz), 0)
    lane = lax.broadcasted_iota(jnp.int32, (width, nz), 1)
    spot = jnp.clip((lane.astype(jnp.float32) + 0.5) * (1.0 / RATIO) - 0.5, 0.0, ez - 1.0)
    weight = jnp.maximum(1.0 - jnp.abs(spot - lax.rem(row, ez).astype(jnp.float32)), 0.0)
    spread_z[...] = weight.astype(jnp.bfloat16)

    for s in range(bx):
        own = [cells[number, s + 1, TOP : TOP + by] for number in (1, 2)]
        for number, part in enumerate(fiber_of(*own)):
            fibers[number, s] = part

    everything(lambda copy: copy.wait_recv(), -1)
    everything(lambda copy: copy.wait_send())


def compute(
    across,
    down,
    sizes,
    cells,
    rest_in,
    held,
    near_slots,
    fibers,
    spread_y,
    spread_z,
    next_potential,
    next_recovery,
    volts,
    conducts,
    out_potential,
    out_recovery,
    out_sem,
):
    bx, by, nz, ex, ey, ez, parts, count = sizes
    blocks = count // LANES
    gx, gy = lax.axis_index("gx"), lax.axis_index("gy")
    first_x, last_x = gx == 0, gx == across - 1
    first_y, last_y = gy == 0, gy == down - 1
    width = (ey + 2) * ez
    tall = by + 8

    for i in range(bx):
        voltage = cells[0, i + 1, TOP : TOP + by]
        resting = rest_in[i]
        out_recovery[i] = resting + 0.05 * (-resting - 8.0 * voltage * (voltage - 1.15))
    leaving = [pltpu.make_async_copy(out_recovery, next_recovery, out_sem.at[bx])]
    leaving[0].start()

    gathered = []
    digits = lax.broadcasted_iota(jnp.int32, (LANES, width), 0)
    pages = down * blocks
    for q in range(3):
        low = jnp.where(first_y, near_slots[q, 1, 0, 0:1], near_slots[q, 0, 0, ey - 1 : ey])
        high = jnp.where(last_y, near_slots[q, 1, 0, ey - 1 : ey], near_slots[q, 2, 0, 0:1])
        pieces = [low] + [near_slots[q, 1, 0, c : c + 1] for c in range(ey)] + [high]
        index = jnp.concatenate(pieces, axis=1) - (gx + q - 1) * (down * count)
        chosen = (digits == (index & (LANES - 1))).astype(jnp.float32).astype(jnp.bfloat16)
        table = [held[q, h, 0 : 8 * blocks] for h in range(down)]
        table += [held[q, h, 8 * blocks : 9 * blocks] for h in range(down)]
        found = dot_two(jnp.concatenate(table, axis=0), chosen)
        page = index >> (LANES.bit_length() - 1)
        total = jnp.zeros((8, width), jnp.float32)
        for h in range(pages):
            total = jnp.where(page == h, found[8 * h : 8 * h + 8], total)
        last = found[8 * pages : 9 * pages]
        kept = lax.broadcasted_iota(jnp.int32, (pages, width), 0) == page
        last = jnp.sum(jnp.where(kept, last, 0.0), axis=0, keepdims=True)
        gathered.append([total, last])
    for part in range(2):
        gathered[0][part] = jnp.where(first_x, gathered[1][part], gathered[0][part])
        gathered[2][part] = jnp.where(last_x, gathered[1][part], gathered[2][part])

    refined = []
    weight_y = spread_y[...]
    weight_z = spread_z[...]
    for q in range(3):
        total, last = gathered[q]
        spread = [weight_y * total[k : k + 1] for k in range(8)] + [weight_y * last]
        refined.append(dot_two(jnp.concatenate(spread, axis=0), weight_z))

    volts[...] = cells[0, :, 0:by + 16]

    @pl.when(first_y)
    def _():
        volts[:, TOP - 1 : TOP] = volts[:, TOP : TOP + 1]

    @pl.when(last_y)
    def _():
        volts[:, TOP + by : TOP + by + 1] = volts[:, TOP + by - 1 : TOP + by]

    @pl.when(first_x)
    def _():
        volts[0] = volts[1]

    @pl.when(last_x)
    def _():
        volts[bx + 1] = volts[bx]

    def rim_of(number):
        rows = [cells[number, s + 1, row : row + 1] for row in (TOP - 1, TOP + by) for s in range(bx)]
        return jnp.concatenate(rows, axis=0)

    rim = [rim_of(1), rim_of(2)]
    rim_fiber = fiber_of(rim[0], rim[1])

    def hat(s):
        spot = (s + 0.5) / RATIO - 0.5
        return [max(0.0, 1.0 - abs(spot - (q - 1))) for q in range(3)]

    for s in range(bx + 2):
        weights = hat(s - 1)
        for half in range(by // 8):
            rows = slice(8 * half, 8 * half + 8)
            entries = []
            for k in range(parts):
                at = tall * k + 8 * half
                terms = [w * refined[q][at : at + 8] for q, w in enumerate(weights) if w]
                entries.append(functools.reduce(jnp.add, terms))
            if 1 <= s <= bx:
                fiber = [fibers[number, s - 1, rows] for number in range(3)]
            else:
                fiber = fiber_of(*(cells[number, s, TOP + 8 * half : TOP + 8 * half + 8] for number in (1, 2)))
            for number, value in enumerate(tensor_of(entries, fiber)):
                conducts[number, s, TOP + 8 * half : TOP + 8 * half + 8] = value
            if 1 <= s <= bx:
                out_potential[s - 1, rows] = stretch_of(entries, fiber)
    rim_row = lax.rem(lax.broadcasted_iota(jnp.int32, (2 * bx, nz), 0), bx).astype(jnp.float32)
    spot = (rim_row + 0.5) * (1.0 / RATIO) - 0.5
    rim_weights = [jnp.maximum(1.0 - jnp.abs(spot - (q - 1.0)), 0.0) for q in range(3)]
    entries = []
    for k in range(parts):
        at = tall * k + by
        entries.append(
            functools.reduce(
                jnp.add, [rim_weights[q] * refined[q][at : at + 2 * bx] for q in range(3)]
            )
        )
    for number, value in enumerate(tensor_of(entries, rim_fiber)):
        for s in range(bx):
            conducts[number, s + 1, TOP - 1 : TOP] = value[s : s + 1]
            conducts[number, s + 1, TOP + by : TOP + by + 1] = value[bx + s : bx + s + 1]

    z_lane = lax.broadcasted_iota(jnp.int32, (by, nz), 1)
    y_row = lax.broadcasted_iota(jnp.int32, (by, nz), 0)

    def next_z(values):
        return jnp.where(z_lane == nz - 1, values, pltpu.roll(values, nz - 1, 1))

    def last_z(values):
        return jnp.where(z_lane == 0, values, pltpu.roll(values, 1, 1))

    def grad_z(values):
        return next_z(values) - last_z(values)

    def at(s, shift):
        return volts[s, TOP + shift : TOP + shift + by]

    def tensor(number, s, shift=0):
        return conducts[number, s, TOP + shift : TOP + shift + by]

    XX, YY, ZZ, XY, XZ, YZ = range(6)
    middle = [at(s, 0) for s in range(bx + 2)]
    grads_y = [at(s, 1) - at(s, -1) for s in range(bx + 2)]
    grads_z = [grad_z(middle[s]) for s in range(bx + 2)]

    def face_x(f):
        def mean(number):
            return tensor(number, f) + tensor(number, f + 1)

        return (
            0.5 * mean(XX) * (middle[f + 1] - middle[f])
            + 0.125 * mean(XY) * (grads_y[f] + grads_y[f + 1])
            + 0.125 * mean(XZ) * (grads_z[f] + grads_z[f + 1])
        )

    faces = [face_x(f) for f in range(bx + 1)]
    faces[0] = jnp.where(first_x, 0.0, faces[0])
    faces[bx] = jnp.where(last_x, 0.0, faces[bx])

    for i in range(bx):
        s = i + 1
        grad_x = middle[s + 1] - middle[s - 1]

        def face_y(shift):
            def mean(number):
                return tensor(number, s) + tensor(number, s, shift)

            step = (at(s, shift) - middle[s]) * (1.0 if shift > 0 else -1.0)
            other_x = at(s + 1, shift) - at(s - 1, shift)
            return (
                0.125 * mean(XY) * (grad_x + other_x)
                + 0.5 * mean(YY) * step
                + 0.125 * mean(YZ) * (grads_z[s] + grad_z(at(s, shift)))
            )

        upper = jnp.where(jnp.logical_and(y_row == by - 1, last_y), 0.0, face_y(1))
        lower = jnp.where(jnp.logical_and(y_row == 0, first_y), 0.0, face_y(-1))

        def pair(values):
            return values + next_z(values)

        face_z = (
            0.125 * pair(tensor(XZ, s)) * pair(grad_x)
            + 0.125 * pair(tensor(YZ, s)) * pair(grads_y[s])
            + 0.5 * pair(tensor(ZZ, s)) * (next_z(middle[s]) - middle[s])
        )
        face_z = jnp.where(z_lane == nz - 1, 0.0, face_z)
        divergent = (
            (faces[i + 1] - faces[i]) + (upper - lower) + (face_z - pltpu.roll(face_z, 1, 1))
        )
        voltage = middle[s]
        resting = rest_in[i]
        current = 8.0 * voltage * (voltage - 0.15) * (voltage - 1.0) + voltage * resting
        current = current + 10.0 * jnp.maximum(out_potential[i] - 1.0, 0.0) * (voltage - 0.6)
        out_potential[i] = voltage + 0.1 * (divergent - current)
        copy = pltpu.make_async_copy(out_potential.at[i], next_potential.at[i], out_sem.at[i])
        copy.start()
        leaving.append(copy)
    for copy in leaving:
        copy.wait()


def solution(mesh):
    across, down = mesh.shape["gx"], mesh.shape["gy"]

    def local(potential, recovery, angles, deform, slots):
        bx, by, nz = potential.shape
        ex, ey, ez = slots.shape
        parts, count = deform.shape
        assert ex == 1 and bx == RATIO and by % 8 == 0 and count % LANES == 0 and parts == 9
        sizes = (bx, by, nz, ex, ey, ez, parts, count)
        blocks = count // LANES
        width = (ey + 2) * ez
        f32 = jnp.float32
        shape = jax.ShapeDtypeStruct(potential.shape, f32)
        anywhere = pl.BlockSpec(memory_space=pl.ANY)
        in_vmem = pl.BlockSpec(memory_space=pltpu.VMEM)
        passed = (
            pltpu.VMEM((3, bx + 2, by + 16, nz), f32),
            pltpu.VMEM(recovery.shape, f32),
            pltpu.VMEM((3, down, 8 * blocks + 8, LANES), f32),
            pltpu.VMEM((3, 3, ex, ey, ez), jnp.int32),
            pltpu.VMEM((3, bx, by, nz), f32),
            pltpu.VMEM((by + 8, width), f32),
            pltpu.VMEM((width, nz), jnp.bfloat16),
        )
        arrived = pl.pallas_call(
            functools.partial(exchange, across, down, sizes),
            out_shape=passed,
            in_specs=[pl.BlockSpec(memory_space=pltpu.MemorySpace.HBM)] * 5,
            out_specs=(in_vmem,) * len(passed),
            scratch_shapes=[
                pltpu.SemaphoreType.DMA((3 * down + 18,)),
                pltpu.SemaphoreType.DMA((3 * down,)),
                pltpu.SemaphoreType.DMA((18,)),
                pltpu.SemaphoreType.DMA((2 * blocks + 4,)),
            ],
            compiler_params=pltpu.CompilerParams(
                collective_id=0, has_side_effects=True, vmem_limit_bytes=VMEM_LIMIT
            ),
        )(*(pltpu.with_memory_space_constraint(x, pltpu.MemorySpace.HBM) for x in (potential, recovery, angles, deform, slots)))
        return pl.pallas_call(
            functools.partial(compute, across, down, sizes),
            out_shape=(shape, shape),
            in_specs=[in_vmem] * len(passed),
            out_specs=(anywhere,) * 2,
            scratch_shapes=[
                pltpu.VMEM((bx + 2, by + 16, nz), f32),
                pltpu.VMEM((6, bx + 2, by + 16, nz), f32),
                pltpu.VMEM((bx, by, nz), f32),
                pltpu.VMEM((bx, by, nz), f32),
                pltpu.SemaphoreType.DMA((bx + 1,)),
            ],
            compiler_params=pltpu.CompilerParams(vmem_limit_bytes=VMEM_LIMIT),
        )(*arrived)

    return jax.shard_map(
        local,
        mesh=mesh,
        in_specs=(
            P("gx", "gy", None),
            P("gx", "gy", None),
            P(None, "gx", "gy", None),
            P(None, ("gx", "gy")),
            P("gx", "gy", None),
        ),
        out_specs=(P("gx", "gy", None), P("gx", "gy", None)),
        check_vma=False,
    )
```

profile of v0, /device:TPU:1, one launch (start us, length us, event | category | flops | bytes accessed | tf_op | source)
XLA Modules:
  0.0 11.3 jit_solution(3959617594519661363)
XLA Ops:
  0.6 8.1 %shard_map.68 = (f32[3,6,32,256]{3,2,1,0:T(8,128)S(1)}, f32[4,16,256]{2,1,0:T(8,128)S(1)}, f32[3,4,24,128]{3,2,1,0:T(8,128)S(1)}, s32[3,3,1,4,64]{4,3,2,1,0:T(4,...) custom-call(f32[4,16,256]{2,1,0:T(8,128)} %potential.1, ...), custom_call_target="tpu_custom_call" | custom-call | tf_op jit(solution)/shard_map/pallas_call | solution.py:493
  8.7 2.5 %shard_map.69 = (f32[4,16,256]{2,1,0:T(8,128)}, f32[4,16,256]{2,1,0:T(8,128)}) custom-call(f32[3,6,32,256]{3,2,1,0:T(8,128)S(1)} %get-tuple-element.9.cells, f32[4,16,256]{2,1,0:T(8,128)S(1)} %get-tuple-element.10.rest_in, f32[3,4,24,128]{3,2,1,0:T(8,128)S(1)} %get-tuple-element.11.held, s32[3,3,1,4,64]{4,3,2,1,0:T(4,128)S(1)} %get-tuple-element.12.near_slots, ...), custom_call_target="tpu_custom_call" | custom-call | tf_op jit(solution)/shard_map/pallas_call | solution.py:508
where the time goes:
time: 11.4 us; the launch traced here: 11.3 us
  Pallas kernels  10.6 us (93%)
  between operations  0.64 us (6%)
    pallas_call x1, Pallas kernels, local(): pl.pallas_call(functools.partial(exchange, across, down, sizes), out_shap...  8.08 us
    pallas_call x1, Pallas kernels, local(): pl.pallas_call(functools.partial(compute, across, down, sizes), out_shape...  2.55 us

commit v1 on v0

--- a/solution.py
+++ b/solution.py
@@ -12,8 +12,6 @@
 LANES = 128
 VMEM_LIMIT = 16 * 1024 * 1024
 TOP = 8
-
-SIDES = tuple((dx, dy) for dx in (-1, 0, 1) for dy in (-1, 0, 1) if (dx, dy) != (0, 0))
 
 
 def split_two(values):
@@ -122,117 +120,145 @@
     spread_z,
     send_sem,
     deform_sem,
-    near_sem,
+    slot_sem,
+    side_sem,
+    edge_sem,
+    corner_sem,
     local_sem,
 ):
     bx, by, nz, ex, ey, ez, parts, count = sizes
     blocks = count // LANES
     gx, gy = lax.axis_index("gx"), lax.axis_index("gy")
-    first_x, last_x = gx == 0, gx == across - 1
     first_y, last_y = gy == 0, gy == down - 1
-
-    def exists(dx, dy):
-        checks = []
-        if dx:
-            checks.append(jnp.logical_not(first_x if dx < 0 else last_x))
-        if dy:
-            checks.append(jnp.logical_not(first_y if dy < 0 else last_y))
-        return checks[0] if len(checks) == 1 else jnp.logical_and(*checks)
+    leave = 2 * lax.rem(gx, 2) - 1
+    sides = []
+    for dx in (leave, -leave):
+        sides.append((dx, jnp.logical_and(gx + dx >= 0, gx + dx < across)))
+
+    def row_targets(include_self):
+        for mask in sorted(range(down), key=lambda m: (-m.bit_count(), m)):
+            if mask == 0 and not include_self:
+                continue
+            if down & (down - 1):
+                yield lax.rem(gy + mask, down)
+            else:
+                target = gy
+                for bit in range(down.bit_length() - 1):
+                    if mask >> bit & 1:
+                        step = 1 << bit
+                        target = target + step - 2 * step * lax.rem(gy // step, 2)
+                yield target
 
     barrier = pltpu.get_barrier_semaphore()
 
-    def row_targets(dx):
-        for step in range(0 if dx else 1, down):
-            yield step, lax.rem(gy + step, down)
-
     def greet(dx):
-        for _, target in row_targets(dx):
+        for target in row_targets(not isinstance(dx, int)):
             pl.semaphore_signal(barrier, inc=1, device_id=(gx + dx, target), device_id_type=MESH)
 
-    pl.when(exists(-1, 0))(lambda: greet(-1))
-    pl.when(exists(1, 0))(lambda: greet(1))
+    for dx, there in sides:
+        pl.when(there)(functools.partial(greet, dx))
     greet(0)
 
     packed = held.at[1, gy]
-    local = []
-
-    def fetch(source, target):
-        copy = pltpu.make_async_copy(source, target, local_sem.at[len(local)])
-        copy.start()
-        local.append(copy)
-
     for b in range(blocks):
         columns = pl.ds(b * LANES, LANES)
-        fetch(deform.at[pl.ds(0, 8), columns], packed.at[pl.ds(8 * b, 8)])
-        fetch(deform.at[pl.ds(8, 1), columns], packed.at[pl.ds(8 * blocks + b, 1)])
-    fetch(slots, near_slots.at[1, 1])
+        pltpu.make_async_copy(
+            deform.at[pl.ds(0, 8), columns], packed.at[pl.ds(8 * b, 8)], local_sem.at[0]
+        ).start()
+        pltpu.make_async_copy(
+            deform.at[pl.ds(8, 1), columns], packed.at[pl.ds(8 * blocks + b, 1)], local_sem.at[0]
+        ).start()
     inside = pl.ds(TOP, by)
-    fetch(potential, cells.at[0, pl.ds(1, bx), inside])
-    fetch(angles, cells.at[pl.ds(1, 2), pl.ds(1, bx), inside])
-    fetch(recovery, rest_in)
-    for copy in local:
-        copy.wait()
-
-    rows_here = 1 + jnp.where(first_x, 0, 1) + jnp.where(last_x, 0, 1)
+    get_slots = pltpu.make_async_copy(slots, near_slots.at[1, 1], local_sem.at[1])
+    get_slots.start()
+    own_cells = cells.at[:, pl.ds(1, bx), inside]
+    pltpu.make_async_copy(potential, cells.at[0, pl.ds(1, bx), inside], local_sem.at[2]).start()
+    pltpu.make_async_copy(angles, cells.at[pl.ds(1, 2), pl.ds(1, bx), inside], local_sem.at[2]).start()
+    get_rest = pltpu.make_async_copy(recovery, rest_in, local_sem.at[3])
+    get_rest.start()
+
+    def drain(ref, sem):
+        pltpu.make_async_copy(ref, ref, sem).wait()
+
+    rows = pl.ds(0, 9 * blocks)
+    drain(held.at[1, gy, rows], local_sem.at[0])
+    rows_here = 1 + sum(there.astype(jnp.int32) for _, there in sides)
     pl.semaphore_wait(barrier, rows_here * down - 1)
 
-    def deform_copy(dx, step, target):
-        index = (1 - dx) * down + step
-        rows = pl.ds(0, 9 * blocks)
+    def put(source, target, sem, dx, where):
         return pltpu.make_async_remote_copy(
-            src_ref=held.at[1, gy, rows],
-            dst_ref=held.at[1 - dx, gy, rows],
-            send_sem=send_sem.at[index],
-            recv_sem=deform_sem.at[index],
-            device_id=(gx + dx, target),
+            src_ref=source,
+            dst_ref=target,
+            send_sem=send_sem.at[0],
+            recv_sem=sem,
+            device_id=(gx + dx, where),
             device_id_type=MESH,
         )
 
-    def near_copies(dx, dy):
-        place = (1 - dx) * 3 + (1 - dy)
-        base = 3 * down + 2 * place
-        x_source = pl.ds(1, bx) if dx == 0 else pl.ds(1 if dx < 0 else bx, 1)
-        x_target = pl.ds(1, bx) if dx == 0 else pl.ds(bx + 1 if dx < 0 else 0, 1)
-        y_source = inside if dy == 0 else pl.ds(TOP if dy < 0 else TOP + by - 1, 1)
-        y_target = inside if dy == 0 else pl.ds(TOP + by if dy < 0 else TOP - 1, 1)
-        fields = pl.ds(0, 1 if dx and dy else 3)
-        pairs = [
-            (near_slots.at[1, 1], near_slots.at[1 - dx, 1 - dy]),
-            (cells.at[fields, x_source, y_source], cells.at[fields, x_target, y_target]),
-        ]
-        return [
-            pltpu.make_async_remote_copy(
-                src_ref=source,
-                dst_ref=target,
-                send_sem=send_sem.at[base + number],
-                recv_sem=near_sem.at[2 * place + number],
-                device_id=(gx + dx, gy + dy),
-                device_id_type=MESH,
-            )
-            for number, (source, target) in enumerate(pairs)
-        ]
-
-    def over_row(dx, act):
-        for step, target in row_targets(dx):
-            act(deform_copy(dx, step, target))
-
-    def over_near(dx, dy, act):
-        for copy in near_copies(dx, dy):
-            act(copy)
-
-    def everything(act, way=1):
-        def side(dx, dy):
-            pl.when(exists(way * dx, way * dy))(lambda: over_near(dx, dy, act))
-
-        for dx in (-1, 1, 0):
-            if dx:
-                pl.when(exists(way * dx, 0))(lambda dx=dx: over_row(dx, act))
-            else:
-                over_row(0, act)
-        for dx, dy in SIDES:
-            side(dx, dy)
-
-    everything(lambda copy: copy.start())
+    def send_deform(dx):
+        q = 1 - dx
+        for target in row_targets(not isinstance(dx, int)):
+            put(held.at[1, gy, rows], held.at[q, gy, rows], deform_sem.at[q], dx, target).start()
+
+    for dx, there in sides:
+        pl.when(there)(functools.partial(send_deform, dx))
+    send_deform(0)
+
+    def at_y(dy, act):
+        pl.when(jnp.logical_not(first_y if dy < 0 else last_y))(act)
+
+    get_slots.wait()
+
+    def send_slots(dx, dy):
+        q = 1 - dx
+        put(near_slots.at[1, 1], near_slots.at[q, 1 - dy], slot_sem.at[q], dx, gy + dy).start()
+
+    def slots_side(dx, straight):
+        if straight:
+            send_slots(dx, 0)
+        for dy in (-1, 1):
+            at_y(dy, functools.partial(send_slots, dx, dy))
+
+    for dx, there in sides:
+        pl.when(there)(functools.partial(slots_side, dx, True))
+    slots_side(0, False)
+
+    drain(own_cells, local_sem.at[2])
+
+    def edges(dy):
+        source = pl.ds(TOP if dy < 0 else TOP + by - 1, 1)
+        target = pl.ds(TOP + by if dy < 0 else TOP - 1, 1)
+        return source, target
+
+    def send_side(dx):
+        q = 1 - dx
+        x_source = pl.ds(jnp.where(dx < 0, 1, bx), 1)
+        x_target = pl.ds(jnp.where(dx < 0, bx + 1, 0), 1)
+        put(cells.at[:, x_source, inside], cells.at[:, x_target, inside], side_sem.at[q // 2], dx, gy).start()
+        for dy in (-1, 1):
+            y_source, y_target = edges(dy)
+
+            def corner(dy=dy, y_source=y_source, y_target=y_target):
+                put(
+                    cells.at[pl.ds(0, 1), x_source, y_source],
+                    cells.at[pl.ds(0, 1), x_target, y_target],
+                    corner_sem.at[q // 2],
+                    dx,
+                    gy + dy,
+                ).start()
+
+            at_y(dy, corner)
+
+    def send_edge(dy):
+        y_source, y_target = edges(dy)
+        x_here = pl.ds(1, bx)
+        put(cells.at[:, x_here, y_source], cells.at[:, x_here, y_target], edge_sem.at[0], 0, gy + dy).start()
+
+    for dx, there in sides:
+        pl.when(there)(functools.partial(send_side, dx))
+    for dy in (-1, 1):
+        at_y(dy, functools.partial(send_edge, dy))
+    get_rest.wait()
 
     width = (ey + 2) * ez
     tall = by + 8
@@ -254,8 +280,47 @@
         for number, part in enumerate(fiber_of(*own)):
             fibers[number, s] = part
 
-    everything(lambda copy: copy.wait_recv(), -1)
-    everything(lambda copy: copy.wait_send())
+    middle_y = jnp.logical_not(jnp.logical_or(first_y, last_y))
+    some_y = jnp.logical_xor(first_y, last_y)
+
+    def over_y(act):
+        pl.when(middle_y)(functools.partial(act, 2))
+        pl.when(some_y)(functools.partial(act, 1))
+
+    def wait_deform(sem, dx):
+        q = 1 - dx
+        part = pl.ds(0, down - 1 if isinstance(dx, int) else down)
+        drain(held.at[q, part, rows], sem if sem is not None else deform_sem.at[q])
+
+    def wait_slots(sem, dx, straight):
+        q = 1 - dx
+        sem = slot_sem.at[q] if sem is None else sem
+        if down == 1:
+            if straight:
+                drain(near_slots.at[1, pl.ds(0, 1)], sem)
+        else:
+            over_y(lambda n: drain(near_slots.at[1, pl.ds(0, n + straight)], sem))
+
+    def wait_side(sem, dx):
+        q = 1 - dx
+        drain(cells.at[:, pl.ds(0, 1), inside], side_sem.at[q // 2] if sem is None else sem)
+        sem = corner_sem.at[q // 2] if sem is None else sem
+        over_y(lambda n: drain(cells.at[pl.ds(0, 1), pl.ds(0, 1), pl.ds(0, n)], sem))
+
+    def wait_all(sem):
+        for dx, there in sides:
+            pl.when(there)(functools.partial(wait_deform, sem, -dx if sem is None else dx))
+        wait_deform(sem, 0)
+        for dx, there in sides:
+            pl.when(there)(functools.partial(wait_slots, sem, -dx if sem is None else dx, 1))
+        wait_slots(sem, 0, 0)
+        for dx, there in sides:
+            pl.when(there)(functools.partial(wait_side, sem, -dx if sem is None else dx))
+        edge = edge_sem.at[0] if sem is None else sem
+        over_y(lambda n: drain(cells.at[:, pl.ds(1, bx), pl.ds(0, n)], edge))
+
+    wait_all(None)
+    wait_all(send_sem.at[0])
 
 
 def compute(
@@ -496,10 +561,13 @@
             in_specs=[pl.BlockSpec(memory_space=pltpu.MemorySpace.HBM)] * 5,
             out_specs=(in_vmem,) * len(passed),
             scratch_shapes=[
-                pltpu.SemaphoreType.DMA((3 * down + 18,)),
-                pltpu.SemaphoreType.DMA((3 * down,)),
-                pltpu.SemaphoreType.DMA((18,)),
-                pltpu.SemaphoreType.DMA((2 * blocks + 4,)),
+                pltpu.SemaphoreType.DMA((1,)),
+                pltpu.SemaphoreType.DMA((3,)),
+                pltpu.SemaphoreType.DMA((3,)),
+                pltpu.SemaphoreType.DMA((2,)),
+                pltpu.SemaphoreType.DMA((1,)),
+                pltpu.SemaphoreType.DMA((2,)),
+                pltpu.SemaphoreType.DMA((4,)),
             ],
             compiler_params=pltpu.CompilerParams(
                 collective_id=0, has_side_effects=True, vmem_limit_bytes=VMEM_LIMIT

time: 11.4 us -> 11.1 us (0.974)
  the two profiles are of different devices: /device:TPU:1 before, /device:TPU:0 now
where the time goes in v1:
time: 11.1 us; the launch traced here: 10.9 us
  Pallas kernels  10.3 us (93%)
  between operations  0.64 us (6%)
    pallas_call x1, Pallas kernels, local(): pl.pallas_call(functools.partial(exchange, across, down, sizes), out_shap...  7.75 us
    pallas_call x1, Pallas kernels, local(): pl.pallas_call(functools.partial(compute, across, down, sizes), out_shape...  2.56 us

profile of v1, /device:TPU:0, one launch (start us, length us, event | category | flops | bytes accessed | tf_op | source)
XLA Modules:
  0.0 10.9 jit_solution(4490618481241053594)
XLA Ops:
  0.6 7.8 %shard_map.68 = (f32[3,6,32,256]{3,2,1,0:T(8,128)S(1)}, f32[4,16,256]{2,1,0:T(8,128)S(1)}, f32[3,4,24,128]{3,2,1,0:T(8,128)S(1)}, s32[3,3,1,4,64]{4,3,2,1,0:T(4,...) custom-call(f32[4,16,256]{2,1,0:T(8,128)} %potential.1, ...), custom_call_target="tpu_custom_call" | custom-call | tf_op jit(solution)/shard_map/pallas_call | solution.py:558
  8.4 2.6 %shard_map.69 = (f32[4,16,256]{2,1,0:T(8,128)}, f32[4,16,256]{2,1,0:T(8,128)}) custom-call(f32[3,6,32,256]{3,2,1,0:T(8,128)S(1)} %get-tuple-element.9.cells, f32[4,16,256]{2,1,0:T(8,128)S(1)} %get-tuple-element.10.rest_in, f32[3,4,24,128]{3,2,1,0:T(8,128)S(1)} %get-tuple-element.11.held, s32[3,3,1,4,64]{4,3,2,1,0:T(4,128)S(1)} %get-tuple-element.12.near_slots, ...), custom_call_target="tpu_custom_call" | custom-call | tf_op jit(solution)/shard_map/pallas_call | solution.py:576

commit v2 on v1

v2 whole, which is shorter than its diff:
```python
import functools

import jax
import jax.numpy as jnp
from jax import lax
from jax.experimental import pallas as pl
from jax.experimental.pallas import tpu as pltpu
from jax.sharding import PartitionSpec as P

MESH = pl.DeviceIdType.MESH
RATIO = 4
LANES = 128
VMEM_LIMIT = 16 * 1024 * 1024
TOP = 8
WINDOW = 4
FIBER_SCALE = (7.0 / 3.0) ** 0.5
STRETCH_SCALE = (3.0 / 7.0) ** 0.5
XX, YY, ZZ, XY, XZ, YZ = range(6)
PAIRS = ((0, 0), (1, 1), (2, 2), (0, 1), (0, 2), (1, 2))


def split_two(values):
    high = values.astype(jnp.bfloat16)
    low = (values - high.astype(jnp.float32)).astype(jnp.bfloat16)
    return high, low


def dot_two(values, weights):
    high, low = split_two(values)
    return jnp.dot(high, weights, preferred_element_type=jnp.float32) + jnp.dot(
        low, weights, preferred_element_type=jnp.float32
    )


def sine_cosine(angle):
    turn = jnp.floor(angle * 0.6366197723675814 + 0.5)
    rest = angle - turn * 1.5703125
    rest = rest - turn * 4.8375129699707031e-4
    rest = rest - turn * 7.549789948768648e-8
    square = rest * rest
    sine = rest + rest * square * (
        -1.6666654611e-1 + square * (8.3321608736e-3 + square * -1.9515295891e-4)
    )
    cosine = (
        1.0
        - 0.5 * square
        + square
        * square
        * (4.166664568298827e-2 + square * (-1.388731625493765e-3 + square * 2.443315711809948e-5))
    )
    size = jnp.abs(turn)
    odd = size == 1.0
    sine_part = jnp.where(odd, cosine * turn, sine)
    cosine_part = jnp.where(odd, sine * -turn, cosine)
    flip = jnp.where(size == 2.0, -1.0, 1.0)
    return sine_part * flip, cosine_part * flip


def fiber_of(azimuth, elevation):
    sin_u, cos_u = sine_cosine(azimuth)
    sin_e, cos_e = sine_cosine(elevation)
    flat = FIBER_SCALE * cos_e
    return cos_u * flat, sin_u * flat, FIBER_SCALE * sin_e


def tensor_of(entries, fiber, sign, wanted):
    def element(i, j):
        return entries[3 * (i % 3) + j % 3]

    adjugate = [
        [
            element(j + 1, i + 1) * element(j + 2, i + 2)
            - element(j + 1, i + 2) * element(j + 2, i + 1)
            for j in range(3)
        ]
        for i in range(3)
    ]
    determinant = (
        element(0, 0) * adjugate[0][0]
        + element(0, 1) * adjugate[1][0]
        + element(0, 2) * adjugate[2][0]
    )
    inverse = 1.0 / determinant
    square = inverse * inverse
    diagonal = (0.3 * 0.5) * square
    mixed = (0.3 * 0.125) * square
    mirrored = (0.3 * 0.125 * sign) * square
    rows = sorted({i for number in wanted for i in PAIRS[number]})
    pulled = {
        i: adjugate[i][0] * fiber[0] + adjugate[i][1] * fiber[1] + adjugate[i][2] * fiber[2]
        for i in rows
    }
    scale = {XX: diagonal, YY: diagonal, ZZ: diagonal, XY: mirrored, XZ: mirrored, YZ: mixed}
    conduct = {}
    for number in wanted:
        i, j = PAIRS[number]
        metric = (
            adjugate[i][0] * adjugate[j][0]
            + adjugate[i][1] * adjugate[j][1]
            + adjugate[i][2] * adjugate[j][2]
        )
        conduct[number] = scale[number] * (metric + pulled[i] * pulled[j])
    return conduct


def excess_of(entries, fiber):
    parts = [
        entries[3 * i] * fiber[0] + entries[3 * i + 1] * fiber[1] + entries[3 * i + 2] * fiber[2]
        for i in range(3)
    ]
    square = parts[0] * parts[0] + parts[1] * parts[1] + parts[2] * parts[2]
    return jnp.maximum(STRETCH_SCALE * (square * lax.rsqrt(square)) - 1.0, 0.0)


class Place:
    def __init__(self, across, down, sizes):
        self.across, self.down, self.sizes = across, down, sizes
        self.gx, self.gy = lax.axis_index("gx"), lax.axis_index("gy")
        self.first_x, self.last_x = self.gx == 0, self.gx == across - 1
        self.first_y, self.last_y = self.gy == 0, self.gy == down - 1
        odd = lax.rem(self.gx, 2)
        self.odd, self.even = odd == 1, odd == 0
        self.leave = 2 * odd - 1
        self.leaves = jnp.logical_not(jnp.logical_or(self.first_x, self.last_x))
        self.late = jnp.where(self.leaves, self.leave, -self.leave)
        self.sign = jnp.where(self.late > 0, 1.0, -1.0)

    def slab(self, j):
        last = self.sizes[0] + 1
        return jnp.where(self.late > 0, j, last - j)


def gather_index(place, near_slots, q, offset):
    ey = place.sizes[4]
    low = jnp.where(place.first_y, near_slots[q, 1, 0, 0:1], near_slots[q, 0, 0, ey - 1 : ey])
    high = jnp.where(place.last_y, near_slots[q, 1, 0, ey - 1 : ey], near_slots[q, 2, 0, 0:1])
    pieces = [low] + [near_slots[q, 1, 0, c : c + 1] for c in range(ey)] + [high]
    count = place.sizes[7]
    return jnp.concatenate(pieces, axis=1) - (place.gx + offset) * (place.down * count)


def gather_row(place, held, q, index):
    blocks = place.sizes[7] // LANES
    pages = place.down * blocks
    width = index.shape[1]
    digits = lax.broadcasted_iota(jnp.int32, (LANES, width), 0)
    chosen = (digits == (index & (LANES - 1))).astype(jnp.float32).astype(jnp.bfloat16)
    table = [held[q, h, 0 : 8 * blocks] for h in range(place.down)]
    table += [held[q, h, 8 * blocks : 9 * blocks] for h in range(place.down)]
    found = dot_two(jnp.concatenate(table, axis=0), chosen)
    page = index >> (LANES.bit_length() - 1)
    total = jnp.zeros((8, width), jnp.float32)
    for h in range(pages):
        total = jnp.where(page == h, found[8 * h : 8 * h + 8], total)
    last = found[8 * pages : 9 * pages]
    kept = lax.broadcasted_iota(jnp.int32, (pages, width), 0) == page
    return total, jnp.sum(jnp.where(kept, last, 0.0), axis=0, keepdims=True)


def refine_row(place, row, weight_y, weight_z):
    by, ez = place.sizes[1], place.sizes[5]
    total, last = row
    span = WINDOW * ez
    spread = []
    for k in range(9):
        values = total[k : k + 1] if k < 8 else last
        for half in range(by // 8):
            at = 2 * half * ez
            spread.append(weight_y[8 * half : 8 * half + 8] * values[:, at : at + span])
        at = (by // 4 - 2) * ez
        rim = lax.broadcasted_iota(jnp.int32, (8, span), 0) < 4
        spread.append(weight_y[by : by + 8] * jnp.where(rim, values[:, 0:span], values[:, at : at + span]))
    return dot_two(jnp.concatenate(spread, axis=0), weight_z)


def rolls(nz, by):
    lane = lax.broadcasted_iota(jnp.int32, (by, nz), 1)

    def ahead(values):
        return pltpu.roll(values, nz - 1, 1)

    def behind(values):
        return pltpu.roll(values, 1, 1)

    return lane, ahead, behind


def grad_z(values):
    nz = values.shape[1]
    lane, ahead, behind = rolls(nz, values.shape[0])
    upper = jnp.where(lane == nz - 1, values, ahead(values))
    lower = jnp.where(lane == 0, values, behind(values))
    return upper - lower


def make_flux(place, volts, slopes, conducts, first):
    by, nz = place.sizes[1], place.sizes[2]
    lane, ahead, behind = rolls(nz, by)
    y_row = lax.broadcasted_iota(jnp.int32, (by, nz), 0)

    def volt(j, shift=0):
        return volts[j, TOP + shift : TOP + shift + by]

    def slope_z(j, shift=0):
        return slopes[j, TOP + shift : TOP + shift + by]

    def tensor(number, j, shift=0):
        return conducts[number, j - first, TOP + shift : TOP + shift + by]

    def slope_y(j):
        return volt(j, 1) - volt(j, -1)

    def slope_x(j, shift=0):
        return volt(j + 1, shift) - volt(j - 1, shift)

    def face_x(j, mine, next_one):
        return (
            (mine[0] + next_one[0]) * (volt(j + 1) - volt(j))
            + (mine[1] + next_one[1]) * (slope_y(j) + slope_y(j + 1))
            + (mine[2] + next_one[2]) * (slope_z(j) + slope_z(j + 1))
        )

    def face_y(j, shift):
        def mean(number):
            return tensor(number, j) + tensor(number, j, shift)

        step = volt(j, shift) - volt(j) if shift > 0 else volt(j) - volt(j, shift)
        return (
            mean(XY) * (slope_x(j) + slope_x(j, shift))
            + mean(YY) * step
            + mean(YZ) * (slope_z(j) + slope_z(j, shift))
        )

    def across_yz(j):
        upper = jnp.where(jnp.logical_and(y_row == by - 1, place.last_y), 0.0, face_y(j, 1))
        lower = jnp.where(jnp.logical_and(y_row == 0, place.first_y), 0.0, face_y(j, -1))

        def pair(values):
            return values + ahead(values)

        face_z = (
            pair(tensor(XZ, j)) * pair(slope_x(j))
            + pair(tensor(YZ, j)) * pair(slope_y(j))
            + pair(tensor(ZZ, j)) * (ahead(volt(j)) - volt(j))
        )
        face_z = jnp.where(lane == nz - 1, 0.0, face_z)
        return (upper - lower) + (face_z - behind(face_z))

    def x_parts(j):
        return [tensor(number, j) for number in (XX, XY, XZ)]

    return face_x, across_yz, x_parts


def put_tensors(place, conducts, slot, mid, side, weight, fiber_at, halo, note):
    by = place.sizes[1]
    tall = by + 8
    for half in range(by // 8):
        rows = slice(8 * half, 8 * half + 8)
        entries = []
        for k in range(9):
            at = tall * k + 8 * half
            base = mid(at)
            entries.append(base + weight * (side(at) - base))
        fiber = fiber_at(rows)
        wanted = (XX, XY, XZ) if halo else tuple(range(6))
        for number, value in tensor_of(entries, fiber, place.sign, wanted).items():
            conducts[number, slot, TOP + 8 * half : TOP + 8 * half + 8] = value
        if not halo:
            note(rows, excess_of(entries, fiber))


def put_rims(place, conducts, slabs, mid, side, rim_fiber):
    bx, by, nz = place.sizes[:3]
    tall = by + 8
    row = lax.rem(lax.broadcasted_iota(jnp.int32, (8, nz), 0), bx)
    weight = jnp.zeros((8, nz), jnp.float32)
    for j in slabs.values():
        weight = jnp.where(row == j - 1, abs((j - 0.5) / RATIO - 0.5), weight)
    entries = []
    for k in range(9):
        base = mid(tall * k + by)
        entries.append(base + weight * (side(tall * k + by) - base))
    for number, value in tensor_of(entries, rim_fiber, place.sign, (YY, XY, YZ)).items():
        for slot, j in slabs.items():
            conducts[number, slot, TOP - 1 : TOP] = value[j - 1 : j]
            conducts[number, slot, TOP + by : TOP + by + 1] = value[bx + j - 1 : bx + j]


def put_volts(place, cells, volts, slopes, j):
    by = place.sizes[1]
    spot = place.slab(j)
    own = cells[0, spot, TOP : TOP + by]
    volts[j, TOP : TOP + by] = own
    low, high = cells[0, spot, TOP - 1 : TOP], cells[0, spot, TOP + by : TOP + by + 1]
    volts[j, TOP - 1 : TOP] = jnp.where(place.first_y, own[0:1], low)
    volts[j, TOP + by : TOP + by + 1] = jnp.where(place.last_y, own[by - 1 : by], high)


def exchange(
    across,
    down,
    sizes,
    potential,
    recovery,
    angles,
    deform,
    slots,
    cells,
    held,
    near_slots,
    fibers,
    rim_fibers,
    spread_y,
    spread_z,
    refined,
    volts,
    slopes,
    edge_tensor,
    partial,
    base,
    next_recovery,
    rest_in,
    conducts,
    early_refined,
    send_sem,
    deform_sem,
    slot_sem,
    side_sem,
    edge_sem,
    corner_sem,
    local_sem,
    plane_sem,
    above_sem,
):
    bx, by, nz, ex, ey, ez, parts, count = sizes
    blocks = count // LANES
    place = Place(across, down, sizes)
    gx, gy = place.gx, place.gy
    first_y, last_y, odd, even, leave = place.first_y, place.last_y, place.odd, place.even, place.leave
    sides = ((leave, place.leaves), (-leave, None))

    def when(check, act):
        if check is None:
            act()
        else:
            pl.when(check)(act)

    def row_targets(include_self=True):
        for mask in sorted(range(down), key=lambda m: (-m.bit_count(), m)):
            if mask == 0 and not include_self:
                continue
            if down & (down - 1):
                yield lax.rem(gy + mask, down)
            else:
                target = gy
                for bit in range(down.bit_length() - 1):
                    if mask >> bit & 1:
                        step = 1 << bit
                        target = target + step - 2 * step * lax.rem(gy // step, 2)
                yield target

    barrier = pltpu.get_barrier_semaphore()

    def tell(sem, row, target):
        pl.semaphore_signal(sem, inc=1, device_id=(row, target), device_id_type=MESH)

    @pl.when(odd)
    def _():
        for target in row_targets(False):
            tell(barrier, gx, target)

        @pl.when(place.leaves)
        def _():
            for target in row_targets():
                tell(barrier, gx + 1, target)

        tell(barrier, gx - 1, gy)

    @pl.when(even)
    def _():
        for target in row_targets():
            tell(barrier, gx + 1, target)

    packed = held.at[1, gy]
    for b in range(blocks):
        columns = pl.ds(b * LANES, LANES)
        pltpu.make_async_copy(
            deform.at[pl.ds(0, 8), columns], packed.at[pl.ds(8 * b, 8)], local_sem.at[0]
        ).start()
        pltpu.make_async_copy(
            deform.at[pl.ds(8, 1), columns], packed.at[pl.ds(8 * blocks + b, 1)], local_sem.at[0]
        ).start()
    inside = pl.ds(TOP, by)
    get_slots = pltpu.make_async_copy(slots, near_slots.at[1, 1], local_sem.at[1])
    get_slots.start()
    own_cells = cells.at[:, pl.ds(1, bx), inside]
    pltpu.make_async_copy(potential, cells.at[0, pl.ds(1, bx), inside], local_sem.at[2]).start()
    pltpu.make_async_copy(angles, cells.at[pl.ds(1, 2), pl.ds(1, bx), inside], local_sem.at[2]).start()
    get_rest = pltpu.make_async_copy(recovery, rest_in, local_sem.at[3])
    get_rest.start()

    def drain(ref, sem):
        pltpu.make_async_copy(ref, ref, sem).wait()

    pl.semaphore_wait(barrier, jnp.where(odd, 2 * down - 1, jnp.where(gx > 0, down + 1, 1)))

    @pl.when(odd)
    def _():
        tell(plane_sem, gx - 1, gy)

    @pl.when(jnp.logical_and(even, place.leaves))
    def _():
        for target in row_targets():
            tell(above_sem, gx - 1, target)

    rows = pl.ds(0, 9 * blocks)
    drain(held.at[1, gy, rows], local_sem.at[0])

    def put(source, target, sem, dx, where):
        pltpu.make_async_remote_copy(
            src_ref=source,
            dst_ref=target,
            send_sem=send_sem.at[0],
            recv_sem=sem,
            device_id=(gx + dx, where),
            device_id_type=MESH,
        ).start()

    def at_y(dy, act):
        pl.when(jnp.logical_not(first_y if dy < 0 else last_y))(act)

    def send_deform(dx):
        q = 1 - dx
        for target in row_targets(not isinstance(dx, int)):
            put(held.at[1, gy, rows], held.at[q, gy, rows], deform_sem.at[q], dx, target)

    def send_slots(dx):
        q = 1 - dx

        def one(dy):
            put(near_slots.at[1, 1], near_slots.at[q, 1 - dy], slot_sem.at[q], dx, gy + dy)

        if not isinstance(dx, int):
            one(0)
        for dy in (-1, 1):
            at_y(dy, functools.partial(one, dy))

    def edges(dy):
        source = pl.ds(TOP if dy < 0 else TOP + by - 1, 1)
        target = pl.ds(TOP + by if dy < 0 else TOP - 1, 1)
        return source, target

    def send_side(dx):
        q = 1 - dx
        x_source = pl.ds(jnp.where(dx < 0, 1, bx), 1)
        x_target = pl.ds(jnp.where(dx < 0, bx + 1, 0), 1)
        put(cells.at[:, x_source, inside], cells.at[:, x_target, inside], side_sem.at[q // 2], dx, gy)

        def corner(dy):
            y_source, y_target = edges(dy)
            source = cells.at[pl.ds(0, 1), x_source, y_source]
            put(source, cells.at[pl.ds(0, 1), x_target, y_target], corner_sem.at[q // 2], dx, gy + dy)

        for dy in (-1, 1):
            at_y(dy, functools.partial(corner, dy))

    def send_edge(dy):
        y_source, y_target = edges(dy)
        x_here = pl.ds(1, bx)
        put(cells.at[:, x_here, y_source], cells.at[:, x_here, y_target], edge_sem.at[0], 0, gy + dy)

    def send_plane():
        send_deform(-leave)
        send_deform(0)
        send_slots(-leave)
        send_slots(0)

    def send_plane_cells():
        send_side(-leave)
        for dy in (-1, 1):
            at_y(dy, functools.partial(send_edge, dy))

    def send_leave():
        send_deform(leave)
        send_slots(leave)

    def local_work():
        width = WINDOW * ez
        row = lax.broadcasted_iota(jnp.int32, (by + 8, width), 0)
        lane = lax.broadcasted_iota(jnp.int32, (by + 8, width), 1)
        low = row < by + bx
        cell = jnp.where(row < by, row, jnp.where(low, -1, by))
        start = jnp.where(row < by, 2 * (row // 8), jnp.where(low, 0, ey - 2))
        spot = (cell.astype(jnp.float32) + 0.5) * (1.0 / RATIO) - 0.5
        coarse = (lane // ez + start - 1).astype(jnp.float32)
        spread_y[...] = jnp.maximum(1.0 - jnp.abs(spot - coarse), 0.0)
        row = lax.broadcasted_iota(jnp.int32, (width, nz), 0)
        lane = lax.broadcasted_iota(jnp.int32, (width, nz), 1)
        spot = jnp.clip((lane.astype(jnp.float32) + 0.5) * (1.0 / RATIO) - 0.5, 0.0, ez - 1.0)
        weight = jnp.maximum(1.0 - jnp.abs(spot - lax.rem(row, ez).astype(jnp.float32)), 0.0)
        spread_z[...] = weight.astype(jnp.bfloat16)
        for s in range(bx):
            own = [cells[number, s + 1, TOP : TOP + by] for number in (1, 2)]
            for number, part in enumerate(fiber_of(*own)):
                fibers[number, s] = part
            voltage = cells[0, s + 1, TOP : TOP + by]
            resting = rest_in[s]
            next_recovery[s] = resting + 0.05 * (-resting - 8.0 * voltage * (voltage - 1.15))
            current = 8.0 * voltage * (voltage - 0.15) * (voltage - 1.0) + voltage * resting
            base[s] = voltage - 0.1 * current

    def stage_odd():
        send_deform(-leave)
        send_deform(0)
        get_slots.wait()
        send_slots(-leave)
        send_slots(0)
        drain(own_cells, local_sem.at[2])
        send_plane_cells()
        get_rest.wait()
        local_work()

        @pl.when(place.leaves)
        def _():
            pl.semaphore_wait(above_sem, down)
            send_leave()
            send_side(leave)

    def stage_even():
        pl.when(place.leaves)(functools.partial(send_deform, leave))
        get_slots.wait()
        pl.when(place.leaves)(functools.partial(send_slots, leave))
        pl.semaphore_wait(plane_sem, 1)
        send_plane()
        drain(own_cells, local_sem.at[2])
        pl.when(place.leaves)(functools.partial(send_side, leave))
        send_plane_cells()
        get_rest.wait()
        local_work()

    pl.when(odd)(stage_odd)
    pl.when(even)(stage_even)

    middle_y = jnp.logical_not(jnp.logical_or(first_y, last_y))
    some_y = jnp.logical_xor(first_y, last_y)

    def over_y(act):
        pl.when(middle_y)(functools.partial(act, 2))
        pl.when(some_y)(functools.partial(act, 1))

    def wait_deform(sem, q, others=0):
        drain(held.at[q, pl.ds(0, down - others), rows], deform_sem.at[q] if sem is None else sem)

    def wait_slots(sem, q, straight=1):
        sem = slot_sem.at[q] if sem is None else sem
        if down == 1:
            if straight:
                drain(near_slots.at[1, pl.ds(0, 1)], sem)
        else:
            over_y(lambda n: drain(near_slots.at[1, pl.ds(0, n + straight)], sem))

    def wait_side(sem, q):
        drain(cells.at[:, pl.ds(0, 1), inside], side_sem.at[q // 2] if sem is None else sem)
        sem = corner_sem.at[q // 2] if sem is None else sem
        over_y(lambda n: drain(cells.at[pl.ds(0, 1), pl.ds(0, 1), pl.ds(0, n)], sem))

    def wait_edge(sem):
        over_y(lambda n: drain(cells.at[:, pl.ds(1, bx), pl.ds(0, n)], sem))

    late = 1 + place.late
    early = 1 - place.late

    def wait_early():
        wait_slots(None, early)
        wait_deform(None, early)
        wait_side(None, early)

    wait_slots(None, 1, 0)
    wait_edge(edge_sem.at[0])
    wait_deform(None, 1, 1)
    pl.when(place.leaves)(wait_early)

    weight_y, weight_z = spread_y[...], spread_z[...]
    middle_row = gather_row(place, held, 1, gather_index(place, near_slots, 1, 0))
    early_row = gather_row(place, held, early, gather_index(place, near_slots, early, -place.late))
    early_row = [jnp.where(place.leaves, a, b) for a, b in zip(early_row, middle_row)]
    refined[...] = refine_row(place, middle_row, weight_y, weight_z)
    early_refined[...] = refine_row(place, early_row, weight_y, weight_z)

    for j in range(bx + 1):
        put_volts(place, cells, volts, slopes, j)

    @pl.when(jnp.logical_not(place.leaves))
    def _():
        volts[0] = volts[1]

    for j in range(bx + 1):
        slopes[j] = grad_z(volts[j])

    def rim_of(number):
        pieces = [cells[number, place.slab(j), row : row + 1] for row in (TOP - 1, TOP + by) for j in range(1, bx + 1)]
        return jnp.concatenate(pieces, axis=0)

    rim_fiber = fiber_of(rim_of(1), rim_of(2))
    for number, value in enumerate(rim_fiber):
        rim_fibers[number] = value

    def mid(at):
        return refined[at : at + 8]

    def side(at):
        return early_refined[at : at + 8]

    half = RATIO // 2
    for j in range(half + 1):
        spot = place.slab(j)

        def fiber_at(rows, j=j, spot=spot):
            if j:
                return [fibers[number, spot - 1, rows] for number in range(3)]
            start = TOP + rows.start
            return fiber_of(*(cells[number, spot, start : start + 8] for number in (1, 2)))

        def note(rows, excess, j=j, spot=spot):
            voltage = volts[j, TOP + rows.start : TOP + rows.stop]
            partial[j - 1, rows] = base[spot - 1, rows] - excess * (voltage - 0.6)

        weight = abs((j - 0.5) / RATIO - 0.5)
        put_tensors(place, conducts, j, mid, side, weight, fiber_at, j == 0, note)
    put_rims(place, conducts, {j: j for j in range(1, half + 1)}, mid, side, rim_fiber)
    face_x, across_yz, x_parts = make_flux(place, volts, slopes, conducts, 0)
    faces = [face_x(j, x_parts(j), x_parts(j + 1)) for j in range(half)]
    faces[0] = jnp.where(place.leaves, faces[0], 0.0)
    partial[0] = partial[0] + 0.1 * (across_yz(1) + (faces[1] - faces[0]))
    partial[1] = partial[1] + 0.1 * (across_yz(2) - faces[1])
    for number, value in enumerate(x_parts(half)):
        edge_tensor[number] = value

    wait_slots(None, late)
    wait_deform(None, late)
    wait_side(None, late)
    out = send_sem.at[0]
    for dx, there in sides:
        when(there, functools.partial(wait_deform, out, 1 - dx))
    wait_deform(out, 1, 1)
    for dx, there in sides:
        when(there, functools.partial(wait_slots, out, 1 - dx))
    wait_slots(out, 1, 0)
    for dx, there in sides:
        when(there, functools.partial(wait_side, out, 1 - dx))
    wait_edge(out)


def compute(
    across,
    down,
    sizes,
    cells,
    held,
    near_slots,
    fibers,
    rim_fibers,
    spread_y,
    spread_z,
    refined,
    volts_in,
    slopes_in,
    edge_tensor,
    partial,
    base,
    recovered,
    next_potential,
    next_recovery,
    volts,
    slopes,
    conducts,
    late_refined,
    result,
    out_sem,
):
    bx, by, nz, ex, ey, ez, parts, count = sizes
    place = Place(across, down, sizes)
    half = RATIO // 2
    late = 1 + place.late

    leaving = [pltpu.make_async_copy(recovered, next_recovery, out_sem.at[0])]
    leaving[0].start()

    def finish(j, source):
        copy = pltpu.make_async_copy(source, next_potential.at[place.slab(j) - 1], out_sem.at[j])
        copy.start()
        leaving.append(copy)

    finish(1, partial.at[0])

    row = gather_row(place, held, late, gather_index(place, near_slots, late, place.late))
    late_refined[...] = refine_row(place, row, spread_y[...], spread_z[...])

    for j in range(half - 1, bx + 1):
        volts[j] = volts_in[j]
        slopes[j] = slopes_in[j]
    put_volts(place, cells, volts, slopes, bx + 1)
    slopes[bx + 1] = grad_z(volts[bx + 1])

    def mid(at):
        return refined[at : at + 8]

    def side(at):
        return late_refined[at : at + 8]

    for j in range(half + 1, bx + 2):
        spot = place.slab(j)

        def fiber_at(rows, j=j, spot=spot):
            if j <= bx:
                return [fibers[number, spot - 1, rows] for number in range(3)]
            start = TOP + rows.start
            return fiber_of(*(cells[number, spot, start : start + 8] for number in (1, 2)))

        def note(rows, excess, j=j, spot=spot):
            voltage = volts[j, TOP + rows.start : TOP + rows.stop]
            result[j - half, rows] = base[spot - 1, rows] - excess * (voltage - 0.6)

        weight = abs((j - 0.5) / RATIO - 0.5)
        put_tensors(place, conducts, j - half - 1, mid, side, weight, fiber_at, j == bx + 1, note)
    rim_fiber = [rim_fibers[number] for number in range(3)]
    put_rims(place, conducts, {j - half - 1: j for j in range(half + 1, bx + 1)}, mid, side, rim_fiber)
    face_x, across_yz, x_parts = make_flux(place, volts, slopes, conducts, half + 1)
    edge = [edge_tensor[number] for number in range(3)]
    faces = {}
    for j in range(half, bx + 1):
        faces[j] = face_x(j, edge if j == half else x_parts(j), x_parts(j + 1))
    result[0] = partial[1] + 0.1 * faces[half]
    finish(half, result.at[0])
    for j in range(half + 1, bx + 1):
        result[j - half] = result[j - half] + 0.1 * (across_yz(j) + (faces[j] - faces[j - 1]))
        finish(j, result.at[j - half])
    for copy in leaving:
        copy.wait()


def solution(mesh):
    across, down = mesh.shape["gx"], mesh.shape["gy"]

    def local(potential, recovery, angles, deform, slots):
        bx, by, nz = potential.shape
        ex, ey, ez = slots.shape
        parts, count = deform.shape
        assert ex == 1 and bx == RATIO and by == RATIO * ey and by % 8 == 0
        assert count % LANES == 0 and parts == 9 and across % 2 == 0 and (2 * ez) % LANES == 0
        sizes = (bx, by, nz, ex, ey, ez, parts, count)
        blocks = count // LANES
        f32 = jnp.float32
        half = RATIO // 2
        shape = jax.ShapeDtypeStruct(potential.shape, f32)
        anywhere = pl.BlockSpec(memory_space=pl.ANY)
        in_vmem = pl.BlockSpec(memory_space=pltpu.VMEM)
        passed = (
            pltpu.VMEM((3, bx + 2, by + 16, nz), f32),
            pltpu.VMEM((3, down, 8 * blocks + 8, LANES), f32),
            pltpu.VMEM((3, 3, ex, ey, ez), jnp.int32),
            pltpu.VMEM((3, bx, by, nz), f32),
            pltpu.VMEM((3, 2 * bx, nz), f32),
            pltpu.VMEM((by + 8, WINDOW * ez), f32),
            pltpu.VMEM((WINDOW * ez, nz), jnp.bfloat16),
            pltpu.VMEM((9 * (by + 8), nz), f32),
            pltpu.VMEM((bx + 1, by + 16, nz), f32),
            pltpu.VMEM((bx + 1, by + 16, nz), f32),
            pltpu.VMEM((3, by, nz), f32),
            pltpu.VMEM((half, by, nz), f32),
            pltpu.VMEM((bx, by, nz), f32),
            pltpu.VMEM((bx, by, nz), f32),
        )
        arrived = pl.pallas_call(
            functools.partial(exchange, across, down, sizes),
            out_shape=passed,
            in_specs=[pl.BlockSpec(memory_space=pltpu.MemorySpace.HBM)] * 5,
            out_specs=(in_vmem,) * len(passed),
            scratch_shapes=[
                pltpu.VMEM(recovery.shape, f32),
                pltpu.VMEM((6, half + 1, by + 16, nz), f32),
                pltpu.VMEM((9 * (by + 8), nz), f32),
                pltpu.SemaphoreType.DMA((1,)),
                pltpu.SemaphoreType.DMA((3,)),
                pltpu.SemaphoreType.DMA((3,)),
                pltpu.SemaphoreType.DMA((2,)),
                pltpu.SemaphoreType.DMA((1,)),
                pltpu.SemaphoreType.DMA((2,)),
                pltpu.SemaphoreType.DMA((4,)),
                pltpu.SemaphoreType.REGULAR,
                pltpu.SemaphoreType.REGULAR,
            ],
            compiler_params=pltpu.CompilerParams(
                collective_id=0, has_side_effects=True, vmem_limit_bytes=VMEM_LIMIT
            ),
        )(*(pltpu.with_memory_space_constraint(x, pltpu.MemorySpace.HBM) for x in (potential, recovery, angles, deform, slots)))
        return pl.pallas_call(
            functools.partial(compute, across, down, sizes),
            out_shape=(shape, shape),
            in_specs=[in_vmem] * len(passed),
            out_specs=(anywhere,) * 2,
            scratch_shapes=[
                pltpu.VMEM((bx + 2, by + 16, nz), f32),
                pltpu.VMEM((bx + 2, by + 16, nz), f32),
                pltpu.VMEM((6, half + 1, by + 16, nz), f32),
                pltpu.VMEM((9 * (by + 8), nz), f32),
                pltpu.VMEM((half + 1, by, nz), f32),
                pltpu.SemaphoreType.DMA((bx + 1,)),
            ],
            compiler_params=pltpu.CompilerParams(vmem_limit_bytes=VMEM_LIMIT),
        )(*arrived)

    return jax.shard_map(
        local,
        mesh=mesh,
        in_specs=(
            P("gx", "gy", None),
            P("gx", "gy", None),
            P(None, "gx", "gy", None),
            P(None, ("gx", "gy")),
            P("gx", "gy", None),
        ),
        out_specs=(P("gx", "gy", None), P("gx", "gy", None)),
        check_vma=False,
    )
```

time: 11.1 us -> 10.9 us (0.982)
  Pallas kernels: 10.3 us -> 10.1 us
    pallas_call x1, Pallas kernels: 2.56 us -> 1.59 us  [local(): pl.pallas_call(functools.partial(compute, across, down, sizes), out_shape...]
    pallas_call x1, Pallas kernels: 7.75 us -> 8.51 us  [local(): pl.pallas_call(functools.partial(exchange, across, down, sizes), out_shap...]
where the time goes in v2:
time: 10.9 us; the launch traced here: 10.7 us
  Pallas kernels  10.1 us (93%)
  between operations  0.64 us (6%)
    pallas_call x1, Pallas kernels, local(): pl.pallas_call(functools.partial(exchange, across, down, sizes), out_shap...  8.51 us
    pallas_call x1, Pallas kernels, local(): pl.pallas_call(functools.partial(compute, across, down, sizes), out_shape...  1.59 us

profile of v2, /device:TPU:0, one launch (start us, length us, event | category | flops | bytes accessed | tf_op | source)
XLA Modules:
  0.0 10.7 jit_solution(15634213039344441631)
XLA Ops:
  0.6 8.5 %shard_map.68 = (f32[3,6,32,256]{3,2,1,0:T(8,128)S(1)}, f32[3,4,24,128]{3,2,1,0:T(8,128)S(1)}, s32[3,3,1,4,64]{4,3,2,1,0:T(4,128)S(1)}, f32[3,4,16,256]{3,2,1,0:...) custom-call(f32[4,16,256]{2,1,0:T(8,128)} %potential.1, ...), custom_call_target="tpu_custom_call" | custom-call | tf_op jit(solution)/shard_map/pallas_call | solution.py:775
  9.2 1.6 %shard_map.69 = (f32[4,16,256]{2,1,0:T(8,128)}, f32[4,16,256]{2,1,0:T(8,128)}) custom-call(f32[3,6,32,256]{3,2,1,0:T(8,128)S(1)} %get-tuple-element.16.cells, f32[3,4,24,128]{3,2,1,0:T(8,128)S(1)} %get-tuple-element.17.held, s32[3,3,1,4,64]{4,3,2,1,0:T(4,128)S(1)} %get-tuple-element.18.near_slots, f32[3,4,16,256]{3,2,1,0:T(8,128)S(1)} %get-tuple-element.19.fibers, ...), custom_call_target="tpu_custom_call" | custom-call | tf_op jit(solution)/shard_map/pallas_call | solution.py:798

commit v3 on v2

--- a/solution.py
+++ b/solution.py
@@ -119,7 +119,6 @@
         self.first_x, self.last_x = self.gx == 0, self.gx == across - 1
         self.first_y, self.last_y = self.gy == 0, self.gy == down - 1
         odd = lax.rem(self.gx, 2)
-        self.odd, self.even = odd == 1, odd == 0
         self.leave = 2 * odd - 1
         self.leaves = jnp.logical_not(jnp.logical_or(self.first_x, self.last_x))
         self.late = jnp.where(self.leaves, self.leave, -self.leave)
@@ -139,25 +138,62 @@
     return jnp.concatenate(pieces, axis=1) - (place.gx + offset) * (place.down * count)
 
 
-def gather_row(place, held, q, index):
+def choose(index):
+    digits = lax.broadcasted_iota(jnp.int32, (LANES, index.shape[1]), 0)
+    return (digits == (index & (LANES - 1))).astype(jnp.float32).astype(jnp.bfloat16)
+
+
+def page_of(index):
+    return index >> (LANES.bit_length() - 1)
+
+
+def keep_page(rows, page):
+    kept = lax.broadcasted_iota(jnp.int32, rows.shape, 0) == page
+    return jnp.sum(jnp.where(kept, rows, 0.0), axis=0, keepdims=True)
+
+
+def gather_row(place, held, q, index, chosen):
     blocks = place.sizes[7] // LANES
     pages = place.down * blocks
-    width = index.shape[1]
-    digits = lax.broadcasted_iota(jnp.int32, (LANES, width), 0)
-    chosen = (digits == (index & (LANES - 1))).astype(jnp.float32).astype(jnp.bfloat16)
     table = [held[q, h, 0 : 8 * blocks] for h in range(place.down)]
     table += [held[q, h, 8 * blocks : 9 * blocks] for h in range(place.down)]
     found = dot_two(jnp.concatenate(table, axis=0), chosen)
-    page = index >> (LANES.bit_length() - 1)
-    total = jnp.zeros((8, width), jnp.float32)
-    for h in range(pages):
+    page = page_of(index)
+    total = found[0:8]
+    for h in range(1, pages):
         total = jnp.where(page == h, found[8 * h : 8 * h + 8], total)
-    last = found[8 * pages : 9 * pages]
-    kept = lax.broadcasted_iota(jnp.int32, (pages, width), 0) == page
-    return total, jnp.sum(jnp.where(kept, last, 0.0), axis=0, keepdims=True)
-
-
-def refine_row(place, row, weight_y, weight_z):
+    return total, keep_page(found[8 * pages : 9 * pages], page)
+
+
+def pick_row(place, held, q, index):
+    blocks = place.sizes[7] // LANES
+    totals, lasts = [], []
+    for t in range(index.shape[1] // LANES):
+        lanes = index[:, t * LANES : (t + 1) * LANES]
+        page = page_of(lanes)
+        spot = jnp.broadcast_to(lanes & (LANES - 1), (8, LANES))
+
+        def take(rows):
+            return jnp.take_along_axis(rows, spot, axis=1, mode="promise_in_bounds")
+
+        total = None
+        tails = []
+        for h in range(place.down):
+            tails.append(held[q, h, 8 * blocks : 9 * blocks])
+            for b in range(blocks):
+                found = take(held[q, h, 8 * b : 8 * b + 8])
+                total = found if total is None else jnp.where(page == h * blocks + b, found, total)
+        totals.append(total)
+        tails = jnp.concatenate(tails, axis=0)
+        last = None
+        for g in range(0, place.down * blocks, 8):
+            part = keep_page(take(tails[g : g + 8]), page - g)
+            last = part if last is None else last + part
+        lasts.append(last)
+    return jnp.concatenate(totals, axis=1), jnp.concatenate(lasts, axis=1)
+
+
+def refine_row(place, row, weight_y, weight_z, whole):
     by, ez = place.sizes[1], place.sizes[5]
     total, last = row
     span = WINDOW * ez
@@ -170,7 +206,10 @@
         at = (by // 4 - 2) * ez
         rim = lax.broadcasted_iota(jnp.int32, (8, span), 0) < 4
         spread.append(weight_y[by : by + 8] * jnp.where(rim, values[:, 0:span], values[:, at : at + span]))
-    return dot_two(jnp.concatenate(spread, axis=0), weight_z)
+    spread = jnp.concatenate(spread, axis=0)
+    if whole:
+        return dot_two(spread, weight_z)
+    return jnp.dot(spread.astype(jnp.bfloat16), weight_z, preferred_element_type=jnp.float32)
 
 
 def rolls(nz, by):
@@ -193,7 +232,7 @@
     return upper - lower
 
 
-def make_flux(place, volts, slopes, conducts, first):
+def make_flux(place, volts, slopes, early, late, first):
     by, nz = place.sizes[1], place.sizes[2]
     lane, ahead, behind = rolls(nz, by)
     y_row = lax.broadcasted_iota(jnp.int32, (by, nz), 0)
@@ -205,7 +244,8 @@
         return slopes[j, TOP + shift : TOP + shift + by]
 
     def tensor(number, j, shift=0):
-        return conducts[number, j - first, TOP + shift : TOP + shift + by]
+        rows = slice(TOP + shift, TOP + shift + by)
+        return early[number, j, rows] if j < first else late[number, j - first, rows]
 
     def slope_y(j):
         return volt(j, 1) - volt(j, -1)
@@ -260,8 +300,7 @@
         entries = []
         for k in range(9):
             at = tall * k + 8 * half
-            base = mid(at)
-            entries.append(base + weight * (side(at) - base))
+            entries.append(mid(at) + weight * side(at))
         fiber = fiber_at(rows)
         wanted = (XX, XY, XZ) if halo else tuple(range(6))
         for number, value in tensor_of(entries, fiber, place.sign, wanted).items():
@@ -279,8 +318,7 @@
         weight = jnp.where(row == j - 1, abs((j - 0.5) / RATIO - 0.5), weight)
     entries = []
     for k in range(9):
-        base = mid(tall * k + by)
-        entries.append(base + weight * (side(tall * k + by) - base))
+        entries.append(mid(tall * k + by) + weight * side(tall * k + by))
     for number, value in tensor_of(entries, rim_fiber, place.sign, (YY, XY, YZ)).items():
         for slot, j in slabs.items():
             conducts[number, slot, TOP - 1 : TOP] = value[j - 1 : j]
@@ -314,30 +352,32 @@
     spread_y,
     spread_z,
     refined,
+    middle,
     volts,
     slopes,
-    edge_tensor,
     partial,
     base,
     next_recovery,
+    conducts,
     rest_in,
-    conducts,
     early_refined,
+    halo_fibers,
+    gauge,
+    slot_gauge,
     send_sem,
     deform_sem,
     slot_sem,
-    side_sem,
-    edge_sem,
-    corner_sem,
+    near_sem,
     local_sem,
-    plane_sem,
-    above_sem,
+    plane_ready,
+    leave_ready,
+    equal_ready,
 ):
     bx, by, nz, ex, ey, ez, parts, count = sizes
     blocks = count // LANES
     place = Place(across, down, sizes)
     gx, gy = place.gx, place.gy
-    first_y, last_y, odd, even, leave = place.first_y, place.last_y, place.odd, place.even, place.leave
+    first_y, last_y, leave = place.first_y, place.last_y, place.leave
     sides = ((leave, place.leaves), (-leave, None))
 
     def when(check, act):
@@ -346,41 +386,71 @@
         else:
             pl.when(check)(act)
 
-    def row_targets(include_self=True):
-        for mask in sorted(range(down), key=lambda m: (-m.bit_count(), m)):
-            if mask == 0 and not include_self:
-                continue
-            if down & (down - 1):
-                yield lax.rem(gy + mask, down)
-            else:
-                target = gy
-                for bit in range(down.bit_length() - 1):
-                    if mask >> bit & 1:
-                        step = 1 << bit
-                        target = target + step - 2 * step * lax.rem(gy // step, 2)
-                yield target
-
-    barrier = pltpu.get_barrier_semaphore()
-
-    def tell(sem, row, target):
-        pl.semaphore_signal(sem, inc=1, device_id=(row, target), device_id_type=MESH)
-
-    @pl.when(odd)
-    def _():
-        for target in row_targets(False):
-            tell(barrier, gx, target)
-
-        @pl.when(place.leaves)
-        def _():
-            for target in row_targets():
-                tell(barrier, gx + 1, target)
-
-        tell(barrier, gx - 1, gy)
-
-    @pl.when(even)
-    def _():
-        for target in row_targets():
-            tell(barrier, gx + 1, target)
+    bits = max(down - 1, 1).bit_length()
+    far = 4 * across * down
+
+    def rank_of(row, column):
+        chip = row // 2
+        if isinstance(column, int):
+            hops = column.bit_count()
+        else:
+            hops = sum(lax.rem(column // (1 << bit), 2) for bit in range(bits))
+        return (chip + hops) * far + chip
+
+    rank = rank_of(gx, gy)
+    columns_by_hops = sorted(range(down), key=lambda column: (column.bit_count(), column))
+
+    def peers(act, groups):
+        for group in groups:
+            rows = ((leave,),) if group else ((-leave, 0),)
+
+            def visit(rows=rows[0]):
+                for column in columns_by_hops:
+                    for dx in rows:
+                        act(dx, column, rank_of(gx + dx, column) - rank)
+
+            when(place.leaves if group else None, visit)
+
+    def other(dx, column):
+        return column != gy if isinstance(dx, int) else True
+
+    def guarded(test, act):
+        def visit(dx, column, above):
+            pl.when(jnp.logical_and(test(above), other(dx, column)))(functools.partial(act, dx, column))
+
+        return visit
+
+    upper_core = lax.rem(gx, 2) == 1
+
+    def meets(row, above, column):
+        even_row = lax.rem(row, 2) == 0
+        return jnp.logical_or(above < 0, jnp.logical_and(above == 0, jnp.logical_or(jnp.logical_not(even_row), column == gy)))
+
+    def lower(act):
+        def visit(dx, column, above):
+            here = jnp.logical_and(meets(gx, above, column), other(dx, column))
+            pl.when(here)(functools.partial(act, dx, column))
+
+        return visit
+
+    def level(act):
+        def visit(dx, column, above):
+            there = jnp.logical_and(meets(gx + dx, -above, column), other(dx, column))
+            pl.when(there)(functools.partial(act, dx, column))
+
+        return visit
+
+    def equal(act):
+        def visit(dx, column, above):
+            pl.when(jnp.logical_and(above == 0, column != gy))(functools.partial(act, dx, column))
+
+        return visit
+
+    def beneath(act):
+        return guarded(lambda above: above < 0, act)
+
+    def higher(act):
+        return guarded(lambda above: above > 0, act)
 
     packed = held.at[1, gy]
     for b in range(blocks):
@@ -392,30 +462,52 @@
             deform.at[pl.ds(8, 1), columns], packed.at[pl.ds(8 * blocks + b, 1)], local_sem.at[0]
         ).start()
     inside = pl.ds(TOP, by)
-    get_slots = pltpu.make_async_copy(slots, near_slots.at[1, 1], local_sem.at[1])
-    get_slots.start()
-    own_cells = cells.at[:, pl.ds(1, bx), inside]
-    pltpu.make_async_copy(potential, cells.at[0, pl.ds(1, bx), inside], local_sem.at[2]).start()
-    pltpu.make_async_copy(angles, cells.at[pl.ds(1, 2), pl.ds(1, bx), inside], local_sem.at[2]).start()
-    get_rest = pltpu.make_async_copy(recovery, rest_in, local_sem.at[3])
-    get_rest.start()
+    pltpu.make_async_copy(slots, near_slots.at[1, 1], local_sem.at[2]).start()
+    pltpu.make_async_copy(potential, cells.at[0, pl.ds(1, bx), inside], local_sem.at[1]).start()
+    pltpu.make_async_copy(angles, cells.at[pl.ds(1, 2), pl.ds(1, bx), inside], local_sem.at[1]).start()
+    pltpu.make_async_copy(recovery, rest_in, local_sem.at[1]).start()
+
+    barrier = pltpu.get_barrier_semaphore()
+
+    def tell(sem, dx, column):
+        pl.semaphore_signal(sem, inc=1, device_id=(gx + dx, column), device_id_type=MESH)
+
+    peers(level(functools.partial(tell, barrier)), (0, 1))
+    below = 0
+    equals = 0
+    plane_above, leave_above = [], []
+    for column in range(down):
+        higher_here = 0
+        for dx in (-leave, 0):
+            above = rank_of(gx + dx, column) - rank
+            below = below + jnp.where(jnp.logical_and(meets(gx, above, column), other(dx, column)), 1, 0)
+            higher_here = higher_here + jnp.where(above > 0, 1, 0)
+            equals = equals + jnp.where(jnp.logical_and(above == 0, column != gy), 1, 0)
+        plane_above.append(higher_here)
+        above = rank_of(gx + leave, column) - rank
+        below = below + jnp.where(jnp.logical_and(place.leaves, meets(gx, above, column)), 1, 0)
+        leave_above.append(jnp.where(jnp.logical_and(place.leaves, above > 0), 1, 0))
+
+    pl.semaphore_wait(barrier, below)
+    pl.when(upper_core)(lambda: tell(equal_ready, -1, gy))
+    peers(beneath(functools.partial(tell, leave_ready.at[gy])), (1,))
+    peers(beneath(functools.partial(tell, plane_ready.at[gy])), (0,))
 
     def drain(ref, sem):
         pltpu.make_async_copy(ref, ref, sem).wait()
 
-    pl.semaphore_wait(barrier, jnp.where(odd, 2 * down - 1, jnp.where(gx > 0, down + 1, 1)))
-
-    @pl.when(odd)
-    def _():
-        tell(plane_sem, gx - 1, gy)
-
-    @pl.when(jnp.logical_and(even, place.leaves))
-    def _():
-        for target in row_targets():
-            tell(above_sem, gx - 1, target)
-
     rows = pl.ds(0, 9 * blocks)
+    line = 4 * nz
+
+    def drain_bytes(amount, sem):
+        assert amount % line == 0
+        drain(gauge.at[pl.ds(0, amount // line)], sem)
+
+    def drain_slots(amount, sem):
+        drain(slot_gauge.at[pl.ds(0, amount)], sem)
+
     drain(held.at[1, gy, rows], local_sem.at[0])
+    drain_slots(1, local_sem.at[2])
 
     def put(source, target, sem, dx, where):
         pltpu.make_async_remote_copy(
@@ -427,63 +519,48 @@
             device_id_type=MESH,
         ).start()
 
-    def at_y(dy, act):
-        pl.when(jnp.logical_not(first_y if dy < 0 else last_y))(act)
-
-    def send_deform(dx):
+    def near_of(dx):
+        return 0 if isinstance(dx, int) else jnp.where(dx == leave, 1, 0)
+
+    def send_deform(dx, column):
         q = 1 - dx
-        for target in row_targets(not isinstance(dx, int)):
-            put(held.at[1, gy, rows], held.at[q, gy, rows], deform_sem.at[q], dx, target)
-
-    def send_slots(dx):
-        q = 1 - dx
-
-        def one(dy):
-            put(near_slots.at[1, 1], near_slots.at[q, 1 - dy], slot_sem.at[q], dx, gy + dy)
-
-        if not isinstance(dx, int):
-            one(0)
-        for dy in (-1, 1):
-            at_y(dy, functools.partial(one, dy))
-
-    def edges(dy):
-        source = pl.ds(TOP if dy < 0 else TOP + by - 1, 1)
-        target = pl.ds(TOP + by if dy < 0 else TOP - 1, 1)
-        return source, target
-
-    def send_side(dx):
-        q = 1 - dx
-        x_source = pl.ds(jnp.where(dx < 0, 1, bx), 1)
-        x_target = pl.ds(jnp.where(dx < 0, bx + 1, 0), 1)
-        put(cells.at[:, x_source, inside], cells.at[:, x_target, inside], side_sem.at[q // 2], dx, gy)
-
-        def corner(dy):
-            y_source, y_target = edges(dy)
-            source = cells.at[pl.ds(0, 1), x_source, y_source]
-            put(source, cells.at[pl.ds(0, 1), x_target, y_target], corner_sem.at[q // 2], dx, gy + dy)
-
-        for dy in (-1, 1):
-            at_y(dy, functools.partial(corner, dy))
-
-    def send_edge(dy):
-        y_source, y_target = edges(dy)
-        x_here = pl.ds(1, bx)
-        put(cells.at[:, x_here, y_source], cells.at[:, x_here, y_target], edge_sem.at[0], 0, gy + dy)
-
-    def send_plane():
-        send_deform(-leave)
-        send_deform(0)
-        send_slots(-leave)
-        send_slots(0)
-
-    def send_plane_cells():
-        send_side(-leave)
-        for dy in (-1, 1):
-            at_y(dy, functools.partial(send_edge, dy))
-
-    def send_leave():
-        send_deform(leave)
-        send_slots(leave)
+        put(held.at[1, gy, rows], held.at[q, gy, rows], deform_sem.at[near_of(dx)], dx, column)
+
+    def send_slots(dx, dy):
+        put(near_slots.at[1, 1], near_slots.at[1 - dx, 1 - dy], slot_sem.at[near_of(dx)], dx, gy + dy)
+
+    def send_cells(dx, dy):
+        y_source = inside if dy == 0 else pl.ds(TOP if dy < 0 else TOP + by - 1, 1)
+        y_target = inside if dy == 0 else pl.ds(TOP + by if dy < 0 else TOP - 1, 1)
+        if isinstance(dx, int):
+            x_source = x_target = pl.ds(1, bx)
+        else:
+            x_source = pl.ds(jnp.where(dx < 0, 1, bx), 1)
+            x_target = pl.ds(jnp.where(dx < 0, bx + 1, 0), 1)
+        corner = dy != 0 and not isinstance(dx, int)
+        fields = pl.ds(0, 1 if corner else 3)
+        source, target = cells.at[fields, x_source, y_source], cells.at[fields, x_target, y_target]
+        put(source, target, near_sem.at[near_of(dx)], dx, gy + dy)
+
+    def neighbours(act, group, sign, column=None):
+        for dx in (leave,) if group else (-leave, 0):
+            for dy in (-1, 0, 1):
+                if isinstance(dx, int) and dy == 0:
+                    continue
+                above = rank_of(gx + dx, gy + dy) - rank
+                if sign > 0:
+                    check = above > 0
+                elif sign < 0:
+                    check = meets(gx, above, gy + dy)
+                else:
+                    check = jnp.logical_and(above == 0, dy != 0)
+                if column is not None:
+                    check = jnp.logical_and(check, gy + dy == column)
+                if dy:
+                    check = jnp.logical_and(check, jnp.logical_not(first_y if dy < 0 else last_y))
+                if group:
+                    check = jnp.logical_and(check, place.leaves)
+                pl.when(check)(functools.partial(act, dx, dy))
 
     def local_work():
         width = WINDOW * ez
@@ -510,84 +587,63 @@
             current = 8.0 * voltage * (voltage - 0.15) * (voltage - 1.0) + voltage * resting
             base[s] = voltage - 0.1 * current
 
-    def stage_odd():
-        send_deform(-leave)
-        send_deform(0)
-        get_slots.wait()
-        send_slots(-leave)
-        send_slots(0)
-        drain(own_cells, local_sem.at[2])
-        send_plane_cells()
-        get_rest.wait()
-        local_work()
-
-        @pl.when(place.leaves)
+    peers(lower(send_deform), (1, 0))
+    for group in (0, 1):
+        neighbours(send_slots, group, -1)
+    drain_bytes(4 * bx * by * line, local_sem.at[1])
+    for group in (1, 0):
+        neighbours(send_cells, group, -1)
+    local_work()
+
+    def send_near(dx, dy):
+        send_slots(dx, dy)
+        send_cells(dx, dy)
+
+    @pl.when(jnp.logical_not(upper_core))
+    def _():
+        pl.semaphore_wait(equal_ready, 1)
+
+        @pl.when(equals > 0)
         def _():
-            pl.semaphore_wait(above_sem, down)
-            send_leave()
-            send_side(leave)
-
-    def stage_even():
-        pl.when(place.leaves)(functools.partial(send_deform, leave))
-        get_slots.wait()
-        pl.when(place.leaves)(functools.partial(send_slots, leave))
-        pl.semaphore_wait(plane_sem, 1)
-        send_plane()
-        drain(own_cells, local_sem.at[2])
-        pl.when(place.leaves)(functools.partial(send_side, leave))
-        send_plane_cells()
-        get_rest.wait()
-        local_work()
-
-    pl.when(odd)(stage_odd)
-    pl.when(even)(stage_even)
+            peers(equal(send_deform), (0,))
+            neighbours(send_near, 0, 0)
+
+    for group, ready, counts in ((0, plane_ready, plane_above), (1, leave_ready, leave_above)):
+        for column in columns_by_hops:
+
+            @pl.when(counts[column] > 0)
+            def _(group=group, ready=ready, counts=counts, column=column):
+                pl.semaphore_wait(ready.at[column], counts[column])
+                for dx in (leave,) if group else (-leave, 0):
+                    higher(send_deform)(dx, column, rank_of(gx + dx, column) - rank)
+                neighbours(send_near, group, 1, column)
 
     middle_y = jnp.logical_not(jnp.logical_or(first_y, last_y))
     some_y = jnp.logical_xor(first_y, last_y)
+    no_y = jnp.logical_and(first_y, last_y)
 
     def over_y(act):
         pl.when(middle_y)(functools.partial(act, 2))
         pl.when(some_y)(functools.partial(act, 1))
-
-    def wait_deform(sem, q, others=0):
-        drain(held.at[q, pl.ds(0, down - others), rows], deform_sem.at[q] if sem is None else sem)
-
-    def wait_slots(sem, q, straight=1):
-        sem = slot_sem.at[q] if sem is None else sem
-        if down == 1:
-            if straight:
-                drain(near_slots.at[1, pl.ds(0, 1)], sem)
-        else:
-            over_y(lambda n: drain(near_slots.at[1, pl.ds(0, n + straight)], sem))
-
-    def wait_side(sem, q):
-        drain(cells.at[:, pl.ds(0, 1), inside], side_sem.at[q // 2] if sem is None else sem)
-        sem = corner_sem.at[q // 2] if sem is None else sem
-        over_y(lambda n: drain(cells.at[pl.ds(0, 1), pl.ds(0, 1), pl.ds(0, n)], sem))
-
-    def wait_edge(sem):
-        over_y(lambda n: drain(cells.at[:, pl.ds(1, bx), pl.ds(0, n)], sem))
+        pl.when(no_y)(functools.partial(act, 0))
+
+    table = 4 * parts * count
+
+    def wait_plane_near(slot, near):
+        over_y(lambda n: drain_slots(2 * n + 1, slot))
+        over_y(lambda n: drain_bytes((3 * by + n * (3 * bx + 1)) * line, near))
+
+    def wait_leave_near(slot, near):
+        over_y(lambda n: drain_slots(n + 1, slot))
+        over_y(lambda n: drain_bytes((3 * by + n) * line, near))
 
     late = 1 + place.late
     early = 1 - place.late
 
-    def wait_early():
-        wait_slots(None, early)
-        wait_deform(None, early)
-        wait_side(None, early)
-
-    wait_slots(None, 1, 0)
-    wait_edge(edge_sem.at[0])
-    wait_deform(None, 1, 1)
-    pl.when(place.leaves)(wait_early)
-
-    weight_y, weight_z = spread_y[...], spread_z[...]
-    middle_row = gather_row(place, held, 1, gather_index(place, near_slots, 1, 0))
-    early_row = gather_row(place, held, early, gather_index(place, near_slots, early, -place.late))
-    early_row = [jnp.where(place.leaves, a, b) for a, b in zip(early_row, middle_row)]
-    refined[...] = refine_row(place, middle_row, weight_y, weight_z)
-    early_refined[...] = refine_row(place, early_row, weight_y, weight_z)
-
+    wait_plane_near(slot_sem.at[0], near_sem.at[0])
+    index_middle = gather_index(place, near_slots, 1, 0)
+    index_early = gather_index(place, near_slots, early, -place.late)
+    chosen_middle, chosen_early = choose(index_middle), choose(index_early)
     for j in range(bx + 1):
         put_volts(place, cells, volts, slopes, j)
 
@@ -602,9 +658,21 @@
         pieces = [cells[number, place.slab(j), row : row + 1] for row in (TOP - 1, TOP + by) for j in range(1, bx + 1)]
         return jnp.concatenate(pieces, axis=0)
 
-    rim_fiber = fiber_of(rim_of(1), rim_of(2))
-    for number, value in enumerate(rim_fiber):
+    for number, value in enumerate(fiber_of(rim_of(1), rim_of(2))):
         rim_fibers[number] = value
+    halo = place.slab(0)
+    for number, value in enumerate(fiber_of(*(cells[n, halo, TOP : TOP + by] for n in (1, 2)))):
+        halo_fibers[number] = value
+
+    drain_bytes((2 * down - 1) * table, deform_sem.at[0])
+    weight_y, weight_z = spread_y[...], spread_z[...]
+    middle_row = gather_row(place, held, 1, index_middle, chosen_middle)
+    early_row = gather_row(place, held, early, index_early, chosen_early)
+    refined[...] = refine_row(place, middle_row, weight_y, weight_z, True)
+    early_row = [jnp.where(place.leaves, a - b, 0.0) for a, b in zip(early_row, middle_row)]
+    early_refined[...] = refine_row(place, early_row, weight_y, weight_z, False)
+    middle[0:8] = middle_row[0]
+    middle[8:9] = middle_row[1]
 
     def mid(at):
         return refined[at : at + 8]
@@ -619,8 +687,7 @@
         def fiber_at(rows, j=j, spot=spot):
             if j:
                 return [fibers[number, spot - 1, rows] for number in range(3)]
-            start = TOP + rows.start
-            return fiber_of(*(cells[number, spot, start : start + 8] for number in (1, 2)))
+            return [halo_fibers[number, rows] for number in range(3)]
 
         def note(rows, excess, j=j, spot=spot):
             voltage = volts[j, TOP + rows.start : TOP + rows.stop]
@@ -628,28 +695,22 @@
 
         weight = abs((j - 0.5) / RATIO - 0.5)
         put_tensors(place, conducts, j, mid, side, weight, fiber_at, j == 0, note)
+    rim_fiber = [rim_fibers[number] for number in range(3)]
     put_rims(place, conducts, {j: j for j in range(1, half + 1)}, mid, side, rim_fiber)
-    face_x, across_yz, x_parts = make_flux(place, volts, slopes, conducts, 0)
-    faces = [face_x(j, x_parts(j), x_parts(j + 1)) for j in range(half)]
-    faces[0] = jnp.where(place.leaves, faces[0], 0.0)
-    partial[0] = partial[0] + 0.1 * (across_yz(1) + (faces[1] - faces[0]))
-    partial[1] = partial[1] + 0.1 * (across_yz(2) - faces[1])
-    for number, value in enumerate(x_parts(half)):
-        edge_tensor[number] = value
-
-    wait_slots(None, late)
-    wait_deform(None, late)
-    wait_side(None, late)
+
     out = send_sem.at[0]
-    for dx, there in sides:
-        when(there, functools.partial(wait_deform, out, 1 - dx))
-    wait_deform(out, 1, 1)
-    for dx, there in sides:
-        when(there, functools.partial(wait_slots, out, 1 - dx))
-    wait_slots(out, 1, 0)
-    for dx, there in sides:
-        when(there, functools.partial(wait_side, out, 1 - dx))
-    wait_edge(out)
+    wait_plane_near(out, out)
+    drain_bytes((2 * down - 1) * table, out)
+
+    @pl.when(place.leaves)
+    def _():
+        wait_leave_near(out, out)
+        drain_bytes(down * table, out)
+
+    @pl.when(place.leaves)
+    def _():
+        wait_leave_near(slot_sem.at[1], near_sem.at[1])
+        drain_bytes(down * table, deform_sem.at[1])
 
 
 def compute(
@@ -664,12 +725,13 @@
     spread_y,
     spread_z,
     refined,
+    middle,
     volts_in,
     slopes_in,
-    edge_tensor,
     partial,
     base,
     recovered,
+    early_conducts,
     next_potential,
     next_recovery,
     volts,
@@ -687,17 +749,16 @@
     leaving = [pltpu.make_async_copy(recovered, next_recovery, out_sem.at[0])]
     leaving[0].start()
 
-    def finish(j, source):
-        copy = pltpu.make_async_copy(source, next_potential.at[place.slab(j) - 1], out_sem.at[j])
+    def finish(j):
+        copy = pltpu.make_async_copy(result.at[j - 1], next_potential.at[place.slab(j) - 1], out_sem.at[j])
         copy.start()
         leaving.append(copy)
 
-    finish(1, partial.at[0])
-
-    row = gather_row(place, held, late, gather_index(place, near_slots, late, place.late))
-    late_refined[...] = refine_row(place, row, spread_y[...], spread_z[...])
-
-    for j in range(half - 1, bx + 1):
+    row = pick_row(place, held, late, gather_index(place, near_slots, late, place.late))
+    row = [a - b for a, b in zip(row, (middle[0:8], middle[8:9]))]
+    late_refined[...] = refine_row(place, row, spread_y[...], spread_z[...], False)
+
+    for j in range(bx + 1):
         volts[j] = volts_in[j]
         slopes[j] = slopes_in[j]
     put_volts(place, cells, volts, slopes, bx + 1)
@@ -720,22 +781,19 @@
 
         def note(rows, excess, j=j, spot=spot):
             voltage = volts[j, TOP + rows.start : TOP + rows.stop]
-            result[j - half, rows] = base[spot - 1, rows] - excess * (voltage - 0.6)
+            result[j - 1, rows] = base[spot - 1, rows] - excess * (voltage - 0.6)
 
         weight = abs((j - 0.5) / RATIO - 0.5)
         put_tensors(place, conducts, j - half - 1, mid, side, weight, fiber_at, j == bx + 1, note)
     rim_fiber = [rim_fibers[number] for number in range(3)]
     put_rims(place, conducts, {j - half - 1: j for j in range(half + 1, bx + 1)}, mid, side, rim_fiber)
-    face_x, across_yz, x_parts = make_flux(place, volts, slopes, conducts, half + 1)
-    edge = [edge_tensor[number] for number in range(3)]
-    faces = {}
-    for j in range(half, bx + 1):
-        faces[j] = face_x(j, edge if j == half else x_parts(j), x_parts(j + 1))
-    result[0] = partial[1] + 0.1 * faces[half]
-    finish(half, result.at[0])
-    for j in range(half + 1, bx + 1):
-        result[j - half] = result[j - half] + 0.1 * (across_yz(j) + (faces[j] - faces[j - 1]))
-        finish(j, result.at[j - half])
+    face_x, across_yz, x_parts = make_flux(place, volts, slopes, early_conducts, conducts, half + 1)
+    faces = [face_x(j, x_parts(j), x_parts(j + 1)) for j in range(bx + 1)]
+    faces[0] = jnp.where(place.leaves, faces[0], 0.0)
+    for j in range(1, bx + 1):
+        local = partial[j - 1] if j <= half else result[j - 1]
+        result[j - 1] = local + 0.1 * (across_yz(j) + (faces[j] - faces[j - 1]))
+        finish(j)
     for copy in leaving:
         copy.wait()
 
@@ -765,12 +823,13 @@
             pltpu.VMEM((by + 8, WINDOW * ez), f32),
             pltpu.VMEM((WINDOW * ez, nz), jnp.bfloat16),
             pltpu.VMEM((9 * (by + 8), nz), f32),
+            pltpu.VMEM((16, (ey + 2) * ez), f32),
             pltpu.VMEM((bx + 1, by + 16, nz), f32),
             pltpu.VMEM((bx + 1, by + 16, nz), f32),
-            pltpu.VMEM((3, by, nz), f32),
             pltpu.VMEM((half, by, nz), f32),
             pltpu.VMEM((bx, by, nz), f32),
             pltpu.VMEM((bx, by, nz), f32),
+            pltpu.VMEM((6, half + 1, by + 16, nz), f32),
         )
         arrived = pl.pallas_call(
             functools.partial(exchange, across, down, sizes),
@@ -779,16 +838,17 @@
             out_specs=(in_vmem,) * len(passed),
             scratch_shapes=[
                 pltpu.VMEM(recovery.shape, f32),
-                pltpu.VMEM((6, half + 1, by + 16, nz), f32),
                 pltpu.VMEM((9 * (by + 8), nz), f32),
-                pltpu.SemaphoreType.DMA((1,)),
-                pltpu.SemaphoreType.DMA((3,)),
-                pltpu.SemaphoreType.DMA((3,)),
-                pltpu.SemaphoreType.DMA((2,)),
+                pltpu.VMEM((3, by, nz), f32),
+                pltpu.VMEM((max(4 * bx * by, 2 * down * parts * count // nz), 1, nz), f32),
+                pltpu.VMEM((5, ex, ey, ez), jnp.int32),
                 pltpu.SemaphoreType.DMA((1,)),
                 pltpu.SemaphoreType.DMA((2,)),
-                pltpu.SemaphoreType.DMA((4,)),
-                pltpu.SemaphoreType.REGULAR,
+                pltpu.SemaphoreType.DMA((2,)),
+                pltpu.SemaphoreType.DMA((2,)),
+                pltpu.SemaphoreType.DMA((3,)),
+                pltpu.SemaphoreType.REGULAR((down,)),
+                pltpu.SemaphoreType.REGULAR((down,)),
                 pltpu.SemaphoreType.REGULAR,
             ],
             compiler_params=pltpu.CompilerParams(
@@ -805,7 +865,7 @@
                 pltpu.VMEM((bx + 2, by + 16, nz), f32),
                 pltpu.VMEM((6, half + 1, by + 16, nz), f32),
                 pltpu.VMEM((9 * (by + 8), nz), f32),
-                pltpu.VMEM((half + 1, by, nz), f32),
+                pltpu.VMEM((bx, by, nz), f32),
                 pltpu.SemaphoreType.DMA((bx + 1,)),
             ],
             compiler_params=pltpu.CompilerParams(vmem_limit_bytes=VMEM_LIMIT),

time: 10.9 us -> 9.97 us (0.915)
  Pallas kernels: 10.1 us -> 9.16 us
    pallas_call x1, Pallas kernels: 8.51 us -> 7.65 us  [local(): pl.pallas_call(functools.partial(exchange, across, down, sizes), out_shap...]
where the time goes in v3:
time: 9.97 us; the launch traced here: 9.8 us
  Pallas kernels  9.16 us (92%)
  between operations  0.64 us (6%)
    pallas_call x1, Pallas kernels, local(): pl.pallas_call(functools.partial(exchange, across, down, sizes), out_shap...  7.65 us
    pallas_call x1, Pallas kernels, local(): pl.pallas_call(functools.partial(compute, across, down, sizes), out_shape...  1.51 us

profile of v3, /device:TPU:0, one launch (start us, length us, event | category | flops | bytes accessed | tf_op | source)
XLA Modules:
  0.0 9.8 jit_solution(6221147222479980841)
XLA Ops:
  0.6 7.7 %shard_map.68 = (f32[3,6,32,256]{3,2,1,0:T(8,128)S(1)}, f32[3,4,24,128]{3,2,1,0:T(8,128)S(1)}, s32[3,3,1,4,64]{4,3,2,1,0:T(4,128)S(1)}, f32[3,4,16,256]{3,2,1,0:...) custom-call(f32[4,16,256]{2,1,0:T(8,128)} %potential.1, ...), custom_call_target="tpu_custom_call" | custom-call | tf_op jit(solution)/shard_map/pallas_call | solution.py:834
  8.3 1.5 %shard_map.69 = (f32[4,16,256]{2,1,0:T(8,128)}, f32[4,16,256]{2,1,0:T(8,128)}) custom-call(f32[3,6,32,256]{3,2,1,0:T(8,128)S(1)} %get-tuple-element.17.cells, f32[3,4,24,128]{3,2,1,0:T(8,128)S(1)} %get-tuple-element.18.held, s32[3,3,1,4,64]{4,3,2,1,0:T(4,128)S(1)} %get-tuple-element.19.near_slots, f32[3,4,16,256]{3,2,1,0:T(8,128)S(1)} %get-tuple-element.20.fibers, ...), custom_call_target="tpu_custom_call" | custom-call | tf_op jit(solution)/shard_map/pallas_call | solution.py:858

commit v4 on v3

v4 whole, which is shorter than its diff:
```python
import functools

import jax
import jax.numpy as jnp
from jax import lax
from jax.experimental import pallas as pl
from jax.experimental.pallas import tpu as pltpu
from jax.sharding import PartitionSpec as P

MESH = pl.DeviceIdType.MESH
RATIO = 4
LANES = 128
VMEM_LIMIT = 16 * 1024 * 1024
TOP = 8
WINDOW = 4
FIBER_SCALE = (7.0 / 3.0) ** 0.5
STRETCH_SCALE = (3.0 / 7.0) ** 0.5
XX, YY, ZZ, XY, XZ, YZ = range(6)
PAIRS = ((0, 0), (1, 1), (2, 2), (0, 1), (0, 2), (1, 2))


def split_two(values):
    high = values.astype(jnp.bfloat16)
    low = (values - high.astype(jnp.float32)).astype(jnp.bfloat16)
    return high, low


def dot_two(values, weights):
    high, low = split_two(values)
    return jnp.dot(high, weights, preferred_element_type=jnp.float32) + jnp.dot(
        low, weights, preferred_element_type=jnp.float32
    )


def polynomial(terms, value):
    total = terms[-1]
    for term in terms[-2::-1]:
        total = total * value + term
    return total


HALF_SINE = (0.707106764632592, -0.02946274890445726, 3.682656229209654e-4, -2.187710743548062e-6, 7.155278665108425e-9)
HALF_COSINE = (1.414213496564441, -0.17677636064176425, 3.6825754039592376e-3, -3.0612650004537585e-5, 1.2790856262670407e-7)


def sine_cosine(angle):
    square = angle * angle
    sine = angle * polynomial(HALF_SINE, square)
    cosine = polynomial(HALF_COSINE, square)
    return sine * cosine, 1.0 - sine * sine


def fiber_of(azimuth, elevation):
    sin_u, cos_u = sine_cosine(azimuth)
    sin_e, cos_e = sine_cosine(elevation)
    flat = FIBER_SCALE * cos_e
    return cos_u * flat, sin_u * flat, FIBER_SCALE * sin_e


def tensor_of(entries, fiber, sign, wanted):
    def element(i, j):
        return entries[3 * (i % 3) + j % 3]

    adjugate = [
        [
            element(j + 1, i + 1) * element(j + 2, i + 2)
            - element(j + 1, i + 2) * element(j + 2, i + 1)
            for j in range(3)
        ]
        for i in range(3)
    ]
    determinant = (
        element(0, 0) * adjugate[0][0]
        + element(0, 1) * adjugate[1][0]
        + element(0, 2) * adjugate[2][0]
    )
    inverse = 1.0 / determinant
    square = inverse * inverse
    diagonal = (0.3 * 0.5) * square
    mixed = (0.3 * 0.125) * square
    mirrored = (0.3 * 0.125 * sign) * square
    rows = sorted({i for number in wanted for i in PAIRS[number]})
    pulled = {
        i: adjugate[i][0] * fiber[0] + adjugate[i][1] * fiber[1] + adjugate[i][2] * fiber[2]
        for i in rows
    }
    scale = {XX: diagonal, YY: diagonal, ZZ: diagonal, XY: mirrored, XZ: mirrored, YZ: mixed}
    conduct = {}
    for number in wanted:
        i, j = PAIRS[number]
        metric = (
            adjugate[i][0] * adjugate[j][0]
            + adjugate[i][1] * adjugate[j][1]
            + adjugate[i][2] * adjugate[j][2]
        )
        conduct[number] = scale[number] * (metric + pulled[i] * pulled[j])
    return conduct


def excess_of(entries, fiber):
    parts = [
        entries[3 * i] * fiber[0] + entries[3 * i + 1] * fiber[1] + entries[3 * i + 2] * fiber[2]
        for i in range(3)
    ]
    square = parts[0] * parts[0] + parts[1] * parts[1] + parts[2] * parts[2]
    return jnp.maximum(STRETCH_SCALE * (square * lax.rsqrt(square)) - 1.0, 0.0)


class Place:
    def __init__(self, across, down, sizes):
        self.across, self.down, self.sizes = across, down, sizes
        self.gx, self.gy = lax.axis_index("gx"), lax.axis_index("gy")
        self.first_x, self.last_x = self.gx == 0, self.gx == across - 1
        self.first_y, self.last_y = self.gy == 0, self.gy == down - 1
        odd = lax.rem(self.gx, 2)
        self.odd = odd
        self.leave = 2 * odd - 1
        self.leaves = jnp.logical_not(jnp.logical_or(self.first_x, self.last_x))
        self.late = jnp.where(self.leaves, self.leave, -self.leave)
        self.sign = jnp.where(self.late > 0, 1.0, -1.0)

    def slab(self, j):
        last = self.sizes[0] + 1
        return jnp.where(self.late > 0, j, last - j)


def load_rows(ref, at, start, size):
    planes = [ref[(*at, part, slice(start, start + size))] for part in range(ref.shape[-3])]
    return jnp.concatenate(planes, axis=1)


def store_rows(ref, at, start, value):
    for part in range(ref.shape[-3]):
        rows = slice(start, start + value.shape[0])
        ref[(*at, part, rows)] = value[:, part * LANES : (part + 1) * LANES]


def gather_index(place, near_slots, q, offset):
    ey = place.sizes[4]
    low = jnp.where(place.first_y, near_slots[q, 1, 0, 0:1], near_slots[q, 0, 0, ey - 1 : ey])
    high = jnp.where(place.last_y, near_slots[q, 1, 0, ey - 1 : ey], near_slots[q, 2, 0, 0:1])
    pieces = [low] + [near_slots[q, 1, 0, c : c + 1] for c in range(ey)] + [high]
    count = place.sizes[7]
    return jnp.concatenate(pieces, axis=1) - (place.gx + offset) * (place.down * count)


def page_of(index):
    return index >> (LANES.bit_length() - 1)


def keep_page(rows, page):
    kept = lax.broadcasted_iota(jnp.int32, rows.shape, 0) == page
    return jnp.sum(jnp.where(kept, rows, 0.0), axis=0, keepdims=True)


def pick_row(place, held, q, index):
    blocks = place.sizes[7] // LANES
    totals, lasts = [], []
    for t in range(index.shape[1] // LANES):
        lanes = index[:, t * LANES : (t + 1) * LANES]
        page = page_of(lanes)
        spot = jnp.broadcast_to(lanes & (LANES - 1), (8, LANES))

        def take(rows):
            return jnp.take_along_axis(rows, spot, axis=1, mode="promise_in_bounds")

        total = None
        tails = []
        for h in range(place.down):
            tails.append(held[q, h, 8 * blocks : 9 * blocks])
            for b in range(blocks):
                found = take(held[q, h, 8 * b : 8 * b + 8])
                total = found if total is None else jnp.where(page == h * blocks + b, found, total)
        totals.append(total)
        tails = jnp.concatenate(tails, axis=0)
        last = None
        for g in range(0, place.down * blocks, 8):
            part = keep_page(take(tails[g : g + 8]), page - g)
            last = part if last is None else last + part
        lasts.append(last)
    return jnp.concatenate(totals, axis=1), jnp.concatenate(lasts, axis=1)


def refine_row(place, row, weight_y, weight_z, whole):
    by, ez = place.sizes[1], place.sizes[5]
    total, last = row
    span = WINDOW * ez
    spread = []
    for k in range(9):
        values = total[k : k + 1] if k < 8 else last
        for half in range(by // 8):
            at = 2 * half * ez
            spread.append(weight_y[8 * half : 8 * half + 8] * values[:, at : at + span])
        at = (by // 4 - 2) * ez
        rim = lax.broadcasted_iota(jnp.int32, (8, span), 0) < 4
        spread.append(weight_y[by : by + 8] * jnp.where(rim, values[:, 0:span], values[:, at : at + span]))
    spread = jnp.concatenate(spread, axis=0)
    if whole:
        return dot_two(spread, weight_z)
    return jnp.dot(spread.astype(jnp.bfloat16), weight_z, preferred_element_type=jnp.float32)


def rolls(nz, by):
    lane = lax.broadcasted_iota(jnp.int32, (by, nz), 1)

    def ahead(values):
        return pltpu.roll(values, nz - 1, 1)

    def behind(values):
        return pltpu.roll(values, 1, 1)

    return lane, ahead, behind


def grad_z(values):
    nz = values.shape[1]
    lane, ahead, behind = rolls(nz, values.shape[0])
    upper = jnp.where(lane == nz - 1, values, ahead(values))
    lower = jnp.where(lane == 0, values, behind(values))
    return upper - lower


class Slopes:
    def __init__(self, place, volts, slopes, parts_x, parts_y, parts_z):
        self.place, self.volts, self.slopes = place, volts, slopes
        self.parts_x, self.parts_y, self.parts_z = parts_x, parts_y, parts_z

    def volt(self, j, shift=0):
        return load_rows(self.volts, (j,), TOP + shift, self.place.sizes[1])

    def slope_z(self, j, shift=0):
        return load_rows(self.slopes, (j,), TOP + shift, self.place.sizes[1])

    def slope_y(self, j):
        return self.volt(j, 1) - self.volt(j, -1)

    def slope_x(self, j, shift=0):
        return self.volt(j + 1, shift) - self.volt(j - 1, shift)

    def pair(self, values):
        return values + pltpu.roll(values, values.shape[1] - 1, 1)

    def along_x(self, j):
        self.parts_x[j, 0] = self.volt(j + 1) - self.volt(j)
        self.parts_x[j, 1] = self.slope_y(j) + self.slope_y(j + 1)
        self.parts_x[j, 2] = self.slope_z(j) + self.slope_z(j + 1)

    def with_x(self, j):
        for side, shift in enumerate((1, -1)):
            self.parts_y[j - 1, side, 0] = self.slope_x(j) + self.slope_x(j, shift)
        self.parts_z[j - 1, 0] = self.pair(self.slope_x(j))

    def within(self, j):
        here = self.volt(j)
        for side, shift in enumerate((1, -1)):
            self.parts_y[j - 1, side, 1] = shift * (self.volt(j, shift) - here)
            self.parts_y[j - 1, side, 2] = self.slope_z(j) + self.slope_z(j, shift)
        self.parts_z[j - 1, 1] = self.pair(self.slope_y(j))
        self.parts_z[j - 1, 2] = pltpu.roll(here, here.shape[1] - 1, 1) - here


def make_flux(place, parts_x, parts_y, parts_z, early, late, first):
    by, nz = place.sizes[1:3]
    lane, ahead, behind = rolls(nz, by)
    y_row = lax.broadcasted_iota(jnp.int32, (by, nz), 0)

    def tensor(number, j, shift=0):
        at = (number, j) if j < first else (number, j - first)
        return load_rows(early if j < first else late, at, TOP + shift, by)

    def face_x(j):
        terms = [
            (tensor(number, j) + tensor(number, j + 1)) * parts_x[j, part]
            for part, number in enumerate((XX, XY, XZ))
        ]
        return terms[0] + terms[1] + terms[2]

    def face_y(j, side, shift):
        terms = [
            (tensor(number, j) + tensor(number, j, shift)) * parts_y[j - 1, side, part]
            for part, number in enumerate((XY, YY, YZ))
        ]
        return terms[0] + terms[1] + terms[2]

    def across_yz(j):
        upper = jnp.where(jnp.logical_and(y_row == by - 1, place.last_y), 0.0, face_y(j, 0, 1))
        lower = jnp.where(jnp.logical_and(y_row == 0, place.first_y), 0.0, face_y(j, 1, -1))
        terms = []
        for part, number in enumerate((XZ, YZ, ZZ)):
            mine = tensor(number, j)
            terms.append((mine + ahead(mine)) * parts_z[j - 1, part])
        face_z = jnp.where(lane == nz - 1, 0.0, terms[0] + terms[1] + terms[2])
        return (upper - lower) + (face_z - behind(face_z))

    return face_x, across_yz


def put_tensors(place, conducts, slot, mid, side, weight, fiber_at, halo, note):
    by = place.sizes[1]
    tall = by + 8
    for half in range(by // 8):
        rows = slice(8 * half, 8 * half + 8)
        entries = []
        for k in range(9):
            at = tall * k + 8 * half
            entries.append(mid(at) + weight * side(at))
        fiber = fiber_at(rows)
        wanted = (XX, XY, XZ) if halo else tuple(range(6))
        for number, value in tensor_of(entries, fiber, place.sign, wanted).items():
            store_rows(conducts, (number, slot), TOP + 8 * half, value)
        if not halo:
            note(rows, excess_of(entries, fiber))


def put_rims(place, conducts, slabs, mid, side, rim_fiber, share):
    bx, by, nz = place.sizes[:3]
    tall = by + 8
    row = lax.rem(lax.broadcasted_iota(jnp.int32, (8, nz), 0), bx)
    weight = jnp.zeros((8, nz), jnp.float32)
    for j in slabs.values():
        weight = jnp.where(row == j - 1, share * abs((j - 0.5) / RATIO - 0.5), weight)
    entries = []
    for k in range(9):
        entries.append(mid(tall * k + by) + weight * side(tall * k + by))
    for number, value in tensor_of(entries, rim_fiber, place.sign, (YY, XY, YZ)).items():
        for slot, j in slabs.items():
            store_rows(conducts, (number, slot), TOP - 1, value[j - 1 : j])
            store_rows(conducts, (number, slot), TOP + by, value[bx + j - 1 : bx + j])


def put_volts(place, cells, volts, slopes, spot, slot):
    by = place.sizes[1]
    own = cells[0, spot, TOP : TOP + by]
    low, high = cells[0, spot, TOP - 1 : TOP], cells[0, spot, TOP + by : TOP + by + 1]
    low = jnp.where(place.first_y, own[0:1], low)
    high = jnp.where(place.last_y, own[by - 1 : by], high)
    for start, value in ((TOP, own), (TOP - 1, low), (TOP + by, high)):
        store_rows(volts, (slot,), start, value)
        store_rows(slopes, (slot,), start, grad_z(value))


def exchange(
    across,
    down,
    sizes,
    potential,
    recovery,
    angles,
    deform,
    slots,
    fibers,
    rim_fibers,
    refined,
    diffs,
    volts,
    slopes,
    parts_x,
    parts_y,
    parts_z,
    partial,
    base,
    next_recovery,
    conducts,
    cells,
    held,
    near_slots,
    rest_in,
    spread_y,
    spread_z,
    middle,
    gauge,
    slot_gauge,
    send_sem,
    deform_sem,
    slot_sem,
    near_sem,
    local_sem,
    plane_ready,
    leave_ready,
    equal_ready,
):
    bx, by, nz, ex, ey, ez, parts, count = sizes
    blocks = count // LANES
    place = Place(across, down, sizes)
    half = RATIO // 2
    gx, gy = place.gx, place.gy
    first_y, last_y, leave = place.first_y, place.last_y, place.leave
    for b in range(blocks):
        columns = pl.ds(b * LANES, LANES)
        pltpu.make_async_copy(
            deform.at[pl.ds(0, 8), columns], held.at[1, gy, pl.ds(8 * b, 8)], local_sem.at[0]
        ).start()
        pltpu.make_async_copy(
            deform.at[pl.ds(8, 1), columns], held.at[1, gy, pl.ds(8 * blocks + b, 1)], local_sem.at[0]
        ).start()
    inside = pl.ds(TOP, by)
    pltpu.make_async_copy(slots, near_slots.at[1, 1], local_sem.at[2]).start()
    pltpu.make_async_copy(potential, cells.at[0, pl.ds(1, bx), inside], local_sem.at[1]).start()
    pltpu.make_async_copy(angles, cells.at[pl.ds(1, 2), pl.ds(1, bx), inside], local_sem.at[1]).start()
    pltpu.make_async_copy(recovery, rest_in, local_sem.at[1]).start()

    sides = ((leave, place.leaves), (-leave, None))

    def when(check, act):
        if check is None:
            act()
        else:
            pl.when(check)(act)

    bits = max(down - 1, 1).bit_length()
    odd = place.odd

    def hops_of(column):
        if isinstance(column, int):
            return column.bit_count()
        hops = 0
        for _ in range(bits):
            halved = column // 2
            hops = hops + column - 2 * halved
            column = halved
        return hops

    own_hops = hops_of(gy)

    def above_of(dx, hops):
        chips = leave if dx is leave else 0
        return 4 * (chips + hops - own_hops) + chips

    columns_by_hops = sorted(range(down), key=lambda column: (column.bit_count(), column))

    def peers(act, groups):
        for group in groups:
            rows = ((leave,),) if group else ((-leave, 0),)

            def visit(rows=rows[0]):
                for column in columns_by_hops:
                    for dx in rows:
                        act(dx, column, above_of(dx, hops_of(column)))

            when(place.leaves if group else None, visit)

    def other(dx, column):
        return column != gy if isinstance(dx, int) else True

    def guarded(test, act):
        def visit(dx, column, above):
            pl.when(jnp.logical_and(test(above), other(dx, column)))(functools.partial(act, dx, column))

        return visit

    upper_core = odd == 1

    def meets(dx, above, column):
        even_row = odd == 0 if isinstance(dx, int) else odd == 1
        return jnp.logical_or(above < 0, jnp.logical_and(above == 0, jnp.logical_or(jnp.logical_not(even_row), column == gy)))

    def lower(act):
        def visit(dx, column, above):
            here = jnp.logical_and(meets(0, above, column), other(dx, column))
            pl.when(here)(functools.partial(act, dx, column))

        return visit

    def level(act):
        def visit(dx, column, above):
            there = jnp.logical_and(meets(dx, -above, column), other(dx, column))
            pl.when(there)(functools.partial(act, dx, column))

        return visit

    def equal(act):
        def visit(dx, column, above):
            pl.when(jnp.logical_and(above == 0, column != gy))(functools.partial(act, dx, column))

        return visit

    def beneath(act):
        return guarded(lambda above: above < 0, act)

    def higher(act):
        return guarded(lambda above: above > 0, act)

    near_hops = {dy: hops_of(gy + dy) for dy in (-1, 0, 1)}
    barrier = pltpu.get_barrier_semaphore()

    def tell(sem, dx, column):
        pl.semaphore_signal(sem, inc=1, device_id=(gx + dx, column), device_id_type=MESH)

    peers(level(functools.partial(tell, barrier)), (0, 1))
    below = 0
    equals = 0
    plane_above, leave_above = [], []
    for column in range(down):
        higher_here = 0
        for dx in (-leave, 0):
            above = above_of(dx, hops_of(column))
            below = below + jnp.where(jnp.logical_and(meets(0, above, column), other(dx, column)), 1, 0)
            higher_here = higher_here + jnp.where(above > 0, 1, 0)
            equals = equals + jnp.where(jnp.logical_and(above == 0, column != gy), 1, 0)
        plane_above.append(higher_here)
        above = above_of(leave, hops_of(column))
        below = below + jnp.where(jnp.logical_and(place.leaves, meets(0, above, column)), 1, 0)
        leave_above.append(jnp.where(jnp.logical_and(place.leaves, above > 0), 1, 0))

    pl.semaphore_wait(barrier, below)
    pl.when(upper_core)(lambda: tell(equal_ready, -1, gy))
    peers(beneath(functools.partial(tell, leave_ready.at[gy])), (1,))
    peers(beneath(functools.partial(tell, plane_ready.at[gy])), (0,))

    def drain(ref, sem):
        pltpu.make_async_copy(ref, ref, sem).wait()

    rows = pl.ds(0, 9 * blocks)
    line = 4 * nz

    def drain_bytes(amount, sem):
        assert amount % line == 0
        drain(gauge.at[pl.ds(0, amount // line)], sem)

    def drain_slots(amount, sem):
        drain(slot_gauge.at[pl.ds(0, amount)], sem)

    drain(held.at[1, gy, rows], local_sem.at[0])
    drain_slots(1, local_sem.at[2])

    def put(source, target, sem, dx, where):
        pltpu.make_async_remote_copy(
            src_ref=source,
            dst_ref=target,
            send_sem=send_sem.at[0],
            recv_sem=sem,
            device_id=(gx + dx, where),
            device_id_type=MESH,
        ).start()

    def near_of(dx):
        return 0 if isinstance(dx, int) else jnp.where(dx == leave, 1, 0)

    def deform_of(dx):
        return 0 if isinstance(dx, int) else jnp.where(dx == leave, 2, 1)

    def send_deform(dx, column):
        q = 1 - dx
        put(held.at[1, gy, rows], held.at[q, gy, rows], deform_sem.at[deform_of(dx)], dx, column)

    def send_slots(dx, dy):
        put(near_slots.at[1, 1], near_slots.at[1 - dx, 1 - dy], slot_sem.at[near_of(dx)], dx, gy + dy)

    def send_cells(dx, dy):
        y_source = inside if dy == 0 else pl.ds(TOP if dy < 0 else TOP + by - 1, 1)
        y_target = inside if dy == 0 else pl.ds(TOP + by if dy < 0 else TOP - 1, 1)
        if isinstance(dx, int):
            x_source = x_target = pl.ds(1, bx)
        else:
            x_source = pl.ds(jnp.where(dx < 0, 1, bx), 1)
            x_target = pl.ds(jnp.where(dx < 0, bx + 1, 0), 1)
        corner = dy != 0 and not isinstance(dx, int)
        fields = pl.ds(0, 1 if corner else 3)
        source, target = cells.at[fields, x_source, y_source], cells.at[fields, x_target, y_target]
        put(source, target, near_sem.at[near_of(dx)], dx, gy + dy)

    def neighbours(act, group, sign, column=None):
        for dx in (leave,) if group else (-leave, 0):
            for dy in (-1, 0, 1):
                if isinstance(dx, int) and dy == 0:
                    continue
                above = above_of(dx, near_hops[dy])
                if sign > 0:
                    check = above > 0
                elif sign < 0:
                    check = meets(0, above, gy + dy)
                else:
                    check = jnp.logical_and(above == 0, dy != 0)
                if column is not None:
                    check = jnp.logical_and(check, gy + dy == column)
                if dy:
                    check = jnp.logical_and(check, jnp.logical_not(first_y if dy < 0 else last_y))
                if group:
                    check = jnp.logical_and(check, place.leaves)
                pl.when(check)(functools.partial(act, dx, dy))

    def local_work():
        width = WINDOW * ez
        row = lax.broadcasted_iota(jnp.int32, (by + 8, width), 0)
        lane = lax.broadcasted_iota(jnp.int32, (by + 8, width), 1)
        low = row < by + bx
        cell = jnp.where(row < by, row, jnp.where(low, -1, by))
        start = jnp.where(row < by, 2 * (row // 8), jnp.where(low, 0, ey - 2))
        spot = (cell.astype(jnp.float32) + 0.5) * (1.0 / RATIO) - 0.5
        coarse = (lane // ez + start - 1).astype(jnp.float32)
        spread_y[...] = jnp.maximum(1.0 - jnp.abs(spot - coarse), 0.0)
        row = lax.broadcasted_iota(jnp.int32, (width, nz), 0)
        lane = lax.broadcasted_iota(jnp.int32, (width, nz), 1)
        spot = jnp.clip((lane.astype(jnp.float32) + 0.5) * (1.0 / RATIO) - 0.5, 0.0, ez - 1.0)
        weight = jnp.maximum(1.0 - jnp.abs(spot - lax.rem(row, ez).astype(jnp.float32)), 0.0)
        spread_z[...] = weight.astype(jnp.bfloat16)
        for s in range(bx):
            own = [cells[number, s + 1, TOP : TOP + by] for number in (1, 2)]
            for number, part in enumerate(fiber_of(*own)):
                fibers[number, s] = part
            voltage = cells[0, s + 1, TOP : TOP + by]
            resting = rest_in[s]
            next_recovery[s] = resting + 0.05 * (-resting - 8.0 * voltage * (voltage - 1.15))
            current = 8.0 * voltage * (voltage - 0.15) * (voltage - 1.0) + voltage * resting
            base[s] = voltage - 0.1 * current

    peers(lower(send_deform), (1, 0))
    for group in (0, 1):
        neighbours(send_slots, group, -1)
    drain_bytes(4 * bx * by * line, local_sem.at[1])
    for group in (1, 0):
        neighbours(send_cells, group, -1)
    local_work()

    def send_near(dx, dy):
        send_slots(dx, dy)
        send_cells(dx, dy)

    @pl.when(jnp.logical_not(upper_core))
    def _():
        pl.semaphore_wait(equal_ready, 1)

        @pl.when(equals > 0)
        def _():
            peers(equal(send_deform), (0,))
            neighbours(send_near, 0, 0)

    for group, ready, counts in ((0, plane_ready, plane_above), (1, leave_ready, leave_above)):
        for column in columns_by_hops:

            @pl.when(counts[column] > 0)
            def _(group=group, ready=ready, counts=counts, column=column):
                pl.semaphore_wait(ready.at[column], counts[column])
                for dx in (leave,) if group else (-leave, 0):
                    higher(send_deform)(dx, column, above_of(dx, hops_of(column)))
                neighbours(send_near, group, 1, column)

    middle_y = jnp.logical_not(jnp.logical_or(first_y, last_y))
    some_y = jnp.logical_xor(first_y, last_y)
    no_y = jnp.logical_and(first_y, last_y)

    def over_y(act):
        pl.when(middle_y)(functools.partial(act, 2))
        pl.when(some_y)(functools.partial(act, 1))
        pl.when(no_y)(functools.partial(act, 0))

    table = 4 * parts * count

    def wait_leave_near(slot, near):
        over_y(lambda n: drain_slots(n + 1, slot))
        over_y(lambda n: drain_bytes((3 * by + n) * line, near))

    def wait_plane_slots(sem):
        over_y(lambda n: drain_slots(2 * n + 1, sem))

    def wait_plane_cells(sem):
        over_y(lambda n: drain_bytes((3 * by + n * (3 * bx + 1)) * line, sem))

    wait_plane_slots(slot_sem.at[0])
    wait_plane_cells(near_sem.at[0])
    drain_bytes((down - 1) * table, deform_sem.at[0])
    drain_bytes(down * table, deform_sem.at[1])
    index_middle = gather_index(place, near_slots, 1, 0)
    index_side = gather_index(place, near_slots, 1 - leave, -leave)
    weight_y, weight_z = spread_y[...], spread_z[...]
    middle_row = pick_row(place, held, 1, index_middle)
    refined[...] = refine_row(place, middle_row, weight_y, weight_z, True)
    middle[0:8] = middle_row[0]
    middle[8:9] = middle_row[1]
    side_row = pick_row(place, held, 1 - leave, index_side)
    side_row = [a - b for a, b in zip(side_row, middle_row)]
    diffs[0] = refine_row(place, side_row, weight_y, weight_z, False)

    for j in range(bx + 1):
        spot = place.slab(j) if j else jnp.where(place.leaves, place.slab(0), place.slab(1))
        put_volts(place, cells, volts, slopes, spot, j)
    slope = Slopes(place, volts, slopes, parts_x, parts_y, parts_z)

    def rim_of(number):
        pieces = [cells[number, place.slab(j), row : row + 1] for row in (TOP - 1, TOP + by) for j in range(1, bx + 1)]
        return jnp.concatenate(pieces, axis=0)

    rim_fiber = fiber_of(rim_of(1), rim_of(2))
    for number, value in enumerate(rim_fiber):
        rim_fibers[number] = value

    def mid(at):
        return refined[at : at + 8]

    def side(at):
        return diffs[0, at : at + 8]

    share = jnp.where(place.leaves, 1.0, 0.0)
    for j in range(half + 1):
        spot = place.slab(j)

        def fiber_at(rows, j=j, spot=spot):
            if j:
                return [fibers[number, spot - 1, rows] for number in range(3)]
            start = TOP + rows.start
            return fiber_of(*(cells[number, spot, start : start + 8] for number in (1, 2)))

        def note(rows, excess, j=j, spot=spot):
            voltage = load_rows(volts, (j,), TOP + rows.start, 8)
            partial[j - 1, rows] = base[spot - 1, rows] - excess * (voltage - 0.6)

        weight = share * abs((j - 0.5) / RATIO - 0.5)
        put_tensors(place, conducts, j, mid, side, weight, fiber_at, j == 0, note)
    put_rims(place, conducts, {j: j for j in range(1, half + 1)}, mid, side, rim_fiber, share)
    for j in range(bx):
        slope.along_x(j)
        slope.within(j + 1)
    for j in range(1, bx):
        slope.with_x(j)

    out = send_sem.at[0]
    wait_plane_slots(out)
    wait_plane_cells(out)
    drain_bytes((2 * down - 1) * table, out)

    @pl.when(place.leaves)
    def _():
        wait_leave_near(out, out)
        drain_bytes(down * table, out)

    @pl.when(place.leaves)
    def _():
        wait_leave_near(slot_sem.at[1], near_sem.at[1])
        index = gather_index(place, near_slots, 1 + leave, leave)
        drain_bytes(down * table, deform_sem.at[2])
        row = pick_row(place, held, 1 + leave, index)
        row = [a - b for a, b in zip(row, (middle[0:8], middle[8:9]))]
        diffs[1] = refine_row(place, row, spread_y[...], spread_z[...], False)


def compute(
    across,
    down,
    sizes,
    fibers,
    rim_fibers,
    refined,
    diffs,
    volts,
    slopes,
    parts_x,
    parts_y,
    parts_z,
    partial,
    base,
    recovered,
    early_conducts,
    cells,
    next_potential,
    next_recovery,
    conducts,
    result,
    out_sem,
):
    bx, by, nz = sizes[:3]
    place = Place(across, down, sizes)
    half = RATIO // 2

    pltpu.make_async_copy(recovered, next_recovery, out_sem.at[0]).start()

    which = jnp.where(place.leaves, 1, 0)
    put_volts(place, cells, volts, slopes, place.slab(bx + 1), bx + 1)
    slope = Slopes(place, volts, slopes, parts_x, parts_y, parts_z)
    slope.along_x(bx)
    slope.with_x(bx)

    def finish(j):
        target = next_potential.at[place.slab(j) - 1]
        pltpu.make_async_copy(result.at[j - 1], target, out_sem.at[0]).start()

    def mid(at):
        return refined[at : at + 8]

    def side(at):
        return diffs[which, at : at + 8]

    for j in range(half + 1, bx + 2):
        spot = place.slab(j)

        def fiber_at(rows, j=j, spot=spot):
            if j <= bx:
                return [fibers[number, spot - 1, rows] for number in range(3)]
            start = TOP + rows.start
            return fiber_of(*(cells[number, spot, start : start + 8] for number in (1, 2)))

        def note(rows, excess, j=j, spot=spot):
            voltage = load_rows(volts, (j,), TOP + rows.start, 8)
            result[j - 1, rows] = base[spot - 1, rows] - excess * (voltage - 0.6)

        weight = abs((j - 0.5) / RATIO - 0.5)
        put_tensors(place, conducts, j - half - 1, mid, side, weight, fiber_at, j == bx + 1, note)
    rim_fiber = [rim_fibers[number] for number in range(3)]
    put_rims(place, conducts, {j - half - 1: j for j in range(half + 1, bx + 1)}, mid, side, rim_fiber, 1.0)
    face_x, across_yz = make_flux(place, parts_x, parts_y, parts_z, early_conducts, conducts, half + 1)
    faces = [face_x(j) for j in range(bx + 1)]
    faces[0] = jnp.where(place.leaves, faces[0], 0.0)
    for j in range(1, bx + 1):
        local = partial[j - 1] if j <= half else result[j - 1]
        result[j - 1] = local + 0.1 * (across_yz(j) + (faces[j] - faces[j - 1]))
        finish(j)
    both = fibers.at[pl.ds(0, 2)]
    pltpu.make_async_copy(both, both, out_sem.at[0]).wait()


def solution(mesh):
    across, down = mesh.shape["gx"], mesh.shape["gy"]

    def local(potential, recovery, angles, deform, slots):
        bx, by, nz = potential.shape
        ex, ey, ez = slots.shape
        parts, count = deform.shape
        assert ex == 1 and bx == RATIO and by == RATIO * ey and by % 8 == 0
        assert count % LANES == 0 and parts == 9 and across % 2 == 0 and (2 * ez) % LANES == 0
        sizes = (bx, by, nz, ex, ey, ez, parts, count)
        blocks = count // LANES
        f32 = jnp.float32
        half = RATIO // 2
        shape = jax.ShapeDtypeStruct(potential.shape, f32)
        anywhere = pl.BlockSpec(memory_space=pl.ANY)
        in_vmem = pl.BlockSpec(memory_space=pltpu.VMEM)
        planes = nz // LANES
        fine = 9 * (by + 8)
        planes = nz // LANES
        fine = 9 * (by + 8)
        rows = pltpu.VMEM((bx + 2, planes, by + 16, LANES), f32)
        passed = (
            pltpu.VMEM((3, bx, by, nz), f32),
            pltpu.VMEM((3, 2 * bx, nz), f32),
            pltpu.VMEM((fine, nz), f32),
            pltpu.VMEM((2, fine, nz), f32),
            rows,
            rows,
            pltpu.VMEM((bx + 1, 3, by, nz), f32),
            pltpu.VMEM((bx, 2, 3, by, nz), f32),
            pltpu.VMEM((bx, 3, by, nz), f32),
            pltpu.VMEM((half, by, nz), f32),
            pltpu.VMEM((bx, by, nz), f32),
            pltpu.VMEM((bx, by, nz), f32),
            pltpu.VMEM((6, half + 1, planes, by + 16, LANES), f32),
            pltpu.VMEM((3, bx + 2, by + 16, nz), f32),
        )
        arrived = pl.pallas_call(
            functools.partial(exchange, across, down, sizes),
            out_shape=passed,
            in_specs=[pl.BlockSpec(memory_space=pltpu.MemorySpace.HBM)] * 5,
            out_specs=(in_vmem,) * len(passed),
            scratch_shapes=[
                pltpu.VMEM((3, down, 8 * blocks + 8, LANES), f32),
                pltpu.VMEM((3, 3, ex, ey, ez), jnp.int32),
                pltpu.VMEM(recovery.shape, f32),
                pltpu.VMEM((by + 8, WINDOW * ez), f32),
                pltpu.VMEM((WINDOW * ez, nz), jnp.bfloat16),
                pltpu.VMEM((16, (ey + 2) * ez), f32),
                pltpu.VMEM((max(4 * bx * by, 2 * down * parts * count // nz), 1, nz), f32),
                pltpu.VMEM((5, ex, ey, ez), jnp.int32),
                pltpu.SemaphoreType.DMA((1,)),
                pltpu.SemaphoreType.DMA((3,)),
                pltpu.SemaphoreType.DMA((2,)),
                pltpu.SemaphoreType.DMA((2,)),
                pltpu.SemaphoreType.DMA((3,)),
                pltpu.SemaphoreType.REGULAR((down,)),
                pltpu.SemaphoreType.REGULAR((down,)),
                pltpu.SemaphoreType.REGULAR,
            ],
            compiler_params=pltpu.CompilerParams(
                collective_id=0, has_side_effects=True, vmem_limit_bytes=VMEM_LIMIT
            ),
        )(*(pltpu.with_memory_space_constraint(x, pltpu.MemorySpace.HBM) for x in (potential, recovery, angles, deform, slots)))
        return pl.pallas_call(
            functools.partial(compute, across, down, sizes),
            out_shape=(shape, shape),
            in_specs=[in_vmem] * len(passed),
            out_specs=(anywhere,) * 2,
            scratch_shapes=[
                pltpu.VMEM((6, half + 1, planes, by + 16, LANES), f32),
                pltpu.VMEM((bx, by, nz), f32),
                pltpu.SemaphoreType.DMA((1,)),
            ],
            compiler_params=pltpu.CompilerParams(vmem_limit_bytes=VMEM_LIMIT),
        )(*arrived)

    return jax.shard_map(
        local,
        mesh=mesh,
        in_specs=(
            P("gx", "gy", None),
            P("gx", "gy", None),
            P(None, "gx", "gy", None),
            P(None, ("gx", "gy")),
            P("gx", "gy", None),
        ),
        out_specs=(P("gx", "gy", None), P("gx", "gy", None)),
        check_vma=False,
    )
```

time: 9.97 us -> 9.59 us (0.962)
  the two profiles are of different devices: /device:TPU:0 before, /device:TPU:1 now
where the time goes in v4:
time: 9.59 us; the launch traced here: 9.42 us
  Pallas kernels  8.78 us (92%)
  between operations  0.64 us (7%)
    pallas_call x1, Pallas kernels, local(): pl.pallas_call(functools.partial(exchange, across, down, sizes), out_shap...  7.71 us
    pallas_call x1, Pallas kernels, local(): pl.pallas_call(functools.partial(compute, across, down, sizes), out_shape...  1.07 us

profile of v4, /device:TPU:1, one launch (start us, length us, event | category | flops | bytes accessed | tf_op | source)
XLA Modules:
  0.0 9.4 jit_solution(13552858498414584720)
XLA Ops:
  0.6 7.7 %shard_map.68 = (f32[3,4,16,256]{3,2,1,0:T(8,128)S(1)}, f32[3,8,256]{2,1,0:T(8,128)S(1)}, f32[216,256]{1,0:T(8,128)S(1)}, f32[2,216,256]{2,1,0:T(8,128)S(1)}, f3...) custom-call(f32[4,16,256]{2,1,0:T(8,128)} %potential.1, ...), custom_call_target="tpu_custom_call" | custom-call | tf_op jit(solution)/shard_map/pallas_call | solution.py:847
  8.3 1.1 %shard_map.69 = (f32[4,16,256]{2,1,0:T(8,128)}, f32[4,16,256]{2,1,0:T(8,128)}) custom-call(f32[3,4,16,256]{3,2,1,0:T(8,128)S(1)} %get-tuple-element.16.fibers, f32[3,8,256]{2,1,0:T(8,128)S(1)} %get-tuple-element.17.rim_fibers, f32[216,256]{1,0:T(8,128)S(1)} %get-tuple-element.18.refined, f32[2,216,256]{2,1,0:T(8,128)S(1)} %get-tuple-element.19.diffs, ...), custom_call_target="tpu_custom_call" | custom-call | tf_op jit(solution)/shard_map/pallas_call | solution.py:874

commit v5 on v4

--- a/solution.py
+++ b/solution.py
@@ -371,7 +371,6 @@
     gauge,
     slot_gauge,
     send_sem,
-    deform_sem,
     slot_sem,
     near_sem,
     local_sem,
@@ -536,12 +535,12 @@
     def near_of(dx):
         return 0 if isinstance(dx, int) else jnp.where(dx == leave, 1, 0)
 
-    def deform_of(dx):
-        return 0 if isinstance(dx, int) else jnp.where(dx == leave, 2, 1)
+    def table_of(dx):
+        return 2 if isinstance(dx, int) else jnp.where(dx == leave, 1, 2)
 
     def send_deform(dx, column):
         q = 1 - dx
-        put(held.at[1, gy, rows], held.at[q, gy, rows], deform_sem.at[deform_of(dx)], dx, column)
+        put(held.at[1, gy, rows], held.at[q, gy, rows], near_sem.at[table_of(dx)], dx, column)
 
     def send_slots(dx, dy):
         put(near_slots.at[1, 1], near_slots.at[1 - dx, 1 - dy], slot_sem.at[near_of(dx)], dx, gy + dy)
@@ -648,20 +647,38 @@
 
     def wait_leave_near(slot, near):
         over_y(lambda n: drain_slots(n + 1, slot))
-        over_y(lambda n: drain_bytes((3 * by + n) * line, near))
+        over_y(lambda n: drain_bytes(down * table + (3 * by + n) * line, near))
 
     def wait_plane_slots(sem):
         over_y(lambda n: drain_slots(2 * n + 1, sem))
 
-    def wait_plane_cells(sem):
+    def wait_plane(sem):
         over_y(lambda n: drain_bytes((3 * by + n * (3 * bx + 1)) * line, sem))
 
     wait_plane_slots(slot_sem.at[0])
-    wait_plane_cells(near_sem.at[0])
-    drain_bytes((down - 1) * table, deform_sem.at[0])
-    drain_bytes(down * table, deform_sem.at[1])
+    wait_plane(near_sem.at[0])
     index_middle = gather_index(place, near_slots, 1, 0)
     index_side = gather_index(place, near_slots, 1 - leave, -leave)
+    for j in range(bx + 1):
+        spot = place.slab(j) if j else jnp.where(place.leaves, place.slab(0), place.slab(1))
+        put_volts(place, cells, volts, slopes, spot, j)
+    slope = Slopes(place, volts, slopes, parts_x, parts_y, parts_z)
+
+    def rim_of(number):
+        pieces = [cells[number, place.slab(j), row : row + 1] for row in (TOP - 1, TOP + by) for j in range(1, bx + 1)]
+        return jnp.concatenate(pieces, axis=0)
+
+    rim_fiber = fiber_of(rim_of(1), rim_of(2))
+    for number, value in enumerate(rim_fiber):
+        rim_fibers[number] = value
+
+    for j in range(bx):
+        slope.along_x(j)
+        slope.within(j + 1)
+    for j in range(1, bx):
+        slope.with_x(j)
+
+    drain_bytes((2 * down - 1) * table, near_sem.at[2])
     weight_y, weight_z = spread_y[...], spread_z[...]
     middle_row = pick_row(place, held, 1, index_middle)
     refined[...] = refine_row(place, middle_row, weight_y, weight_z, True)
@@ -671,19 +688,6 @@
     side_row = [a - b for a, b in zip(side_row, middle_row)]
     diffs[0] = refine_row(place, side_row, weight_y, weight_z, False)
 
-    for j in range(bx + 1):
-        spot = place.slab(j) if j else jnp.where(place.leaves, place.slab(0), place.slab(1))
-        put_volts(place, cells, volts, slopes, spot, j)
-    slope = Slopes(place, volts, slopes, parts_x, parts_y, parts_z)
-
-    def rim_of(number):
-        pieces = [cells[number, place.slab(j), row : row + 1] for row in (TOP - 1, TOP + by) for j in range(1, bx + 1)]
-        return jnp.concatenate(pieces, axis=0)
-
-    rim_fiber = fiber_of(rim_of(1), rim_of(2))
-    for number, value in enumerate(rim_fiber):
-        rim_fibers[number] = value
-
     def mid(at):
         return refined[at : at + 8]
 
@@ -691,46 +695,42 @@
         return diffs[0, at : at + 8]
 
     share = jnp.where(place.leaves, 1.0, 0.0)
-    for j in range(half + 1):
+    def early_slab(j):
         spot = place.slab(j)
 
-        def fiber_at(rows, j=j, spot=spot):
+        def fiber_at(rows):
             if j:
                 return [fibers[number, spot - 1, rows] for number in range(3)]
             start = TOP + rows.start
             return fiber_of(*(cells[number, spot, start : start + 8] for number in (1, 2)))
 
-        def note(rows, excess, j=j, spot=spot):
+        def note(rows, excess):
             voltage = load_rows(volts, (j,), TOP + rows.start, 8)
             partial[j - 1, rows] = base[spot - 1, rows] - excess * (voltage - 0.6)
 
         weight = share * abs((j - 0.5) / RATIO - 0.5)
         put_tensors(place, conducts, j, mid, side, weight, fiber_at, j == 0, note)
+
+    for j in range(1, half + 1):
+        early_slab(j)
     put_rims(place, conducts, {j: j for j in range(1, half + 1)}, mid, side, rim_fiber, share)
-    for j in range(bx):
-        slope.along_x(j)
-        slope.within(j + 1)
-    for j in range(1, bx):
-        slope.with_x(j)
-
     out = send_sem.at[0]
     wait_plane_slots(out)
-    wait_plane_cells(out)
+    wait_plane(out)
     drain_bytes((2 * down - 1) * table, out)
 
     @pl.when(place.leaves)
     def _():
         wait_leave_near(out, out)
-        drain_bytes(down * table, out)
 
     @pl.when(place.leaves)
     def _():
         wait_leave_near(slot_sem.at[1], near_sem.at[1])
         index = gather_index(place, near_slots, 1 + leave, leave)
-        drain_bytes(down * table, deform_sem.at[2])
         row = pick_row(place, held, 1 + leave, index)
         row = [a - b for a, b in zip(row, (middle[0:8], middle[8:9]))]
         diffs[1] = refine_row(place, row, spread_y[...], spread_z[...], False)
+        early_slab(0)
 
 
 def compute(
@@ -856,12 +856,11 @@
                 pltpu.VMEM((by + 8, WINDOW * ez), f32),
                 pltpu.VMEM((WINDOW * ez, nz), jnp.bfloat16),
                 pltpu.VMEM((16, (ey + 2) * ez), f32),
-                pltpu.VMEM((max(4 * bx * by, 2 * down * parts * count // nz), 1, nz), f32),
+                pltpu.VMEM((4 * bx * by + 2 * down * parts * count // nz, 1, nz), f32),
                 pltpu.VMEM((5, ex, ey, ez), jnp.int32),
                 pltpu.SemaphoreType.DMA((1,)),
+                pltpu.SemaphoreType.DMA((2,)),
                 pltpu.SemaphoreType.DMA((3,)),
-                pltpu.SemaphoreType.DMA((2,)),
-                pltpu.SemaphoreType.DMA((2,)),
                 pltpu.SemaphoreType.DMA((3,)),
                 pltpu.SemaphoreType.REGULAR((down,)),
                 pltpu.SemaphoreType.REGULAR((down,)),

time: 9.59 us -> 9.45 us (0.985)
  Pallas kernels: 8.78 us -> 8.63 us
    pallas_call x1, Pallas kernels: 7.71 us -> 7.56 us  [local(): pl.pallas_call(functools.partial(exchange, across, down, sizes), out_shap...]
where the time goes in v5:
time: 9.45 us; the launch traced here: 9.27 us
  Pallas kernels  8.63 us (91%)
  between operations  0.64 us (7%)
    pallas_call x1, Pallas kernels, local(): pl.pallas_call(functools.partial(exchange, across, down, sizes), out_shap...  7.56 us
    pallas_call x1, Pallas kernels, local(): pl.pallas_call(functools.partial(compute, across, down, sizes), out_shape...  1.07 us

profile of v5, /device:TPU:1, one launch (start us, length us, event | category | flops | bytes accessed | tf_op | source)
XLA Modules:
  0.0 9.3 jit_solution(12942128474176784343)
XLA Ops:
  0.6 7.6 %shard_map.68 = (f32[3,4,16,256]{3,2,1,0:T(8,128)S(1)}, f32[3,8,256]{2,1,0:T(8,128)S(1)}, f32[216,256]{1,0:T(8,128)S(1)}, f32[2,216,256]{2,1,0:T(8,128)S(1)}, f3...) custom-call(f32[4,16,256]{2,1,0:T(8,128)} %potential.1, ...), custom_call_target="tpu_custom_call" | custom-call | tf_op jit(solution)/shard_map/pallas_call | solution.py:847
  8.2 1.1 %shard_map.69 = (f32[4,16,256]{2,1,0:T(8,128)}, f32[4,16,256]{2,1,0:T(8,128)}) custom-call(f32[3,4,16,256]{3,2,1,0:T(8,128)S(1)} %get-tuple-element.16.fibers, f32[3,8,256]{2,1,0:T(8,128)S(1)} %get-tuple-element.17.rim_fibers, f32[216,256]{1,0:T(8,128)S(1)} %get-tuple-element.18.refined, f32[2,216,256]{2,1,0:T(8,128)S(1)} %get-tuple-element.19.diffs, ...), custom_call_target="tpu_custom_call" | custom-call | tf_op jit(solution)/shard_map/pallas_call | solution.py:873

commit v6 on v5

--- a/solution.py
+++ b/solution.py
@@ -438,12 +438,26 @@
 
             when(place.leaves if group else None, visit)
 
+    relayed = down == 4
+
+    def apart(dx, column):
+        if not relayed or dx is not leave or column not in (0, down - 1):
+            return True
+        here = jnp.logical_and(odd == 1, gy == down - 1) if column == 0 else jnp.logical_and(odd == 0, gy == 0)
+        return jnp.logical_not(here)
+
+    relays_table = jnp.logical_and(place.leaves, jnp.logical_and(odd == 1, gy == down - 1)) if relayed else False
+    sends_less = jnp.logical_and(place.leaves, jnp.logical_and(odd == 1, gy == down - 1))
+    forwards = jnp.logical_and(place.leaves, jnp.logical_and(odd == 1, gy == 0))
+    announces = jnp.logical_and(gx >= 3, jnp.logical_and(odd == 1, gy == 0))
+
     def other(dx, column):
         return column != gy if isinstance(dx, int) else True
 
     def guarded(test, act):
         def visit(dx, column, above):
-            pl.when(jnp.logical_and(test(above), other(dx, column)))(functools.partial(act, dx, column))
+            here = jnp.logical_and(test(above), other(dx, column))
+            pl.when(here)(functools.partial(act, dx, column))
 
         return visit
 
@@ -455,14 +469,14 @@
 
     def lower(act):
         def visit(dx, column, above):
-            here = jnp.logical_and(meets(0, above, column), other(dx, column))
+            here = jnp.logical_and(meets(0, above, column), jnp.logical_and(other(dx, column), apart(dx, column)))
             pl.when(here)(functools.partial(act, dx, column))
 
         return visit
 
     def level(act):
         def visit(dx, column, above):
-            there = jnp.logical_and(meets(dx, -above, column), other(dx, column))
+            there = jnp.logical_and(meets(dx, -above, column), jnp.logical_and(other(dx, column), apart(dx, column)))
             pl.when(there)(functools.partial(act, dx, column))
 
         return visit
@@ -474,7 +488,10 @@
         return visit
 
     def beneath(act):
-        return guarded(lambda above: above < 0, act)
+        def visit(dx, column, above):
+            pl.when(jnp.logical_and(above < 0, apart(dx, column)))(functools.partial(act, dx, column))
+
+        return visit
 
     def higher(act):
         return guarded(lambda above: above > 0, act)
@@ -498,10 +515,16 @@
             equals = equals + jnp.where(jnp.logical_and(above == 0, column != gy), 1, 0)
         plane_above.append(higher_here)
         above = above_of(leave, hops_of(column))
-        below = below + jnp.where(jnp.logical_and(place.leaves, meets(0, above, column)), 1, 0)
+        met = jnp.logical_and(meets(0, above, column), apart(leave, column))
+        below = below + jnp.where(jnp.logical_and(place.leaves, met), 1, 0)
         leave_above.append(jnp.where(jnp.logical_and(place.leaves, above > 0), 1, 0))
 
+    if relayed:
+        below = below + jnp.where(announces, 1, 0)
+        pl.when(sends_less)(lambda: tell(barrier, 2, 0))
     pl.semaphore_wait(barrier, below)
+    if relayed:
+        pl.when(announces)(lambda: tell(leave_ready.at[down - 1], -1, 0))
     pl.when(upper_core)(lambda: tell(equal_ready, -1, gy))
     peers(beneath(functools.partial(tell, leave_ready.at[gy])), (1,))
     peers(beneath(functools.partial(tell, plane_ready.at[gy])), (0,))
@@ -535,12 +558,14 @@
     def near_of(dx):
         return 0 if isinstance(dx, int) else jnp.where(dx == leave, 1, 0)
 
-    def table_of(dx):
-        return 2 if isinstance(dx, int) else jnp.where(dx == leave, 1, 2)
+    def table_of(dx, column):
+        if isinstance(dx, int):
+            return jnp.where(relays_table, 3, 2) if column == 0 else 2
+        return jnp.where(dx == leave, 1, 2)
 
     def send_deform(dx, column):
         q = 1 - dx
-        put(held.at[1, gy, rows], held.at[q, gy, rows], near_sem.at[table_of(dx)], dx, column)
+        put(held.at[1, gy, rows], held.at[q, gy, rows], near_sem.at[table_of(dx, column)], dx, column)
 
     def send_slots(dx, dy):
         put(near_slots.at[1, 1], near_slots.at[1 - dx, 1 - dy], slot_sem.at[near_of(dx)], dx, gy + dy)
@@ -568,6 +593,8 @@
                     check = above > 0
                 elif sign < 0:
                     check = meets(0, above, gy + dy)
+                    if dy:
+                        check = jnp.logical_and(check, above < 0)
                 else:
                     check = jnp.logical_and(above == 0, dy != 0)
                 if column is not None:
@@ -603,26 +630,50 @@
             current = 8.0 * voltage * (voltage - 0.15) * (voltage - 1.0) + voltage * resting
             base[s] = voltage - 0.1 * current
 
-    peers(lower(send_deform), (1, 0))
-    for group in (0, 1):
-        neighbours(send_slots, group, -1)
-    drain_bytes(4 * bx * by * line, local_sem.at[1])
-    for group in (1, 0):
-        neighbours(send_cells, group, -1)
-    local_work()
-
     def send_near(dx, dy):
         send_slots(dx, dy)
         send_cells(dx, dy)
 
+    def wait_cells():
+        drain_bytes(4 * bx * by * line, local_sem.at[1])
+
+    meets_equals = jnp.logical_and(upper_core, equals > 0)
+
+    def split_equals(strict):
+        def visit(dx, column, above):
+            test = above < 0 if strict else above == 0
+            lower(lambda *peer: pl.when(test)(functools.partial(send_deform, *peer)))(dx, column, above)
+
+        return visit
+
+    @pl.when(meets_equals)
+    def _():
+        wait_cells()
+        for group in (0, 1):
+            neighbours(send_near, group, -1)
+
+    pl.when(meets_equals)(lambda: neighbours(send_near, 0, 0))
+    peers(split_equals(False), (0,))
+    peers(split_equals(True), (1, 0))
+
+    @pl.when(jnp.logical_not(meets_equals))
+    def _():
+        for group in (0, 1):
+            neighbours(send_slots, group, -1)
+        wait_cells()
+        for group in (1, 0):
+            neighbours(send_cells, group, -1)
+
+    local_work()
+
     @pl.when(jnp.logical_not(upper_core))
     def _():
         pl.semaphore_wait(equal_ready, 1)
 
         @pl.when(equals > 0)
         def _():
+            neighbours(send_near, 0, 0)
             peers(equal(send_deform), (0,))
-            neighbours(send_near, 0, 0)
 
     for group, ready, counts in ((0, plane_ready, plane_above), (1, leave_ready, leave_above)):
         for column in columns_by_hops:
@@ -645,9 +696,9 @@
 
     table = 4 * parts * count
 
-    def wait_leave_near(slot, near):
+    def wait_leave_near(slot, near, tables=down):
         over_y(lambda n: drain_slots(n + 1, slot))
-        over_y(lambda n: drain_bytes(down * table + (3 * by + n) * line, near))
+        over_y(lambda n: drain_bytes(tables * table + (3 * by + n) * line, near))
 
     def wait_plane_slots(sem):
         over_y(lambda n: drain_slots(2 * n + 1, sem))
@@ -655,10 +706,15 @@
     def wait_plane(sem):
         over_y(lambda n: drain_bytes((3 * by + n * (3 * bx + 1)) * line, sem))
 
-    wait_plane_slots(slot_sem.at[0])
+    if relayed:
+
+        @pl.when(forwards)
+        def _():
+            drain_bytes(table, near_sem.at[3])
+            source = held.at[1, down - 1, rows]
+            put(source, held.at[0, down - 1, rows], near_sem.at[1], leave, 0)
+
     wait_plane(near_sem.at[0])
-    index_middle = gather_index(place, near_slots, 1, 0)
-    index_side = gather_index(place, near_slots, 1 - leave, -leave)
     for j in range(bx + 1):
         spot = place.slab(j) if j else jnp.where(place.leaves, place.slab(0), place.slab(1))
         put_volts(place, cells, volts, slopes, spot, j)
@@ -678,7 +734,14 @@
     for j in range(1, bx):
         slope.with_x(j)
 
-    drain_bytes((2 * down - 1) * table, near_sem.at[2])
+    wait_plane_slots(slot_sem.at[0])
+    if relayed:
+        pl.when(jnp.logical_not(forwards))(lambda: drain_bytes((2 * down - 1) * table, near_sem.at[2]))
+        pl.when(forwards)(lambda: drain_bytes((2 * down - 2) * table, near_sem.at[2]))
+    else:
+        drain_bytes((2 * down - 1) * table, near_sem.at[2])
+    index_middle = gather_index(place, near_slots, 1, 0)
+    index_side = gather_index(place, near_slots, 1 - leave, -leave)
     weight_y, weight_z = spread_y[...], spread_z[...]
     middle_row = pick_row(place, held, 1, index_middle)
     refined[...] = refine_row(place, middle_row, weight_y, weight_z, True)
@@ -721,7 +784,12 @@
 
     @pl.when(place.leaves)
     def _():
-        wait_leave_near(out, out)
+        wait_leave_near(out, out, down - 1)
+        if relayed:
+            pl.when(jnp.logical_not(sends_less))(lambda: drain_bytes(table, out))
+            pl.when(forwards)(lambda: drain_bytes(table, out))
+        else:
+            drain_bytes(table, out)
 
     @pl.when(place.leaves)
     def _():
@@ -860,7 +928,7 @@
                 pltpu.VMEM((5, ex, ey, ez), jnp.int32),
                 pltpu.SemaphoreType.DMA((1,)),
                 pltpu.SemaphoreType.DMA((2,)),
-                pltpu.SemaphoreType.DMA((3,)),
+                pltpu.SemaphoreType.DMA((4,)),
                 pltpu.SemaphoreType.DMA((3,)),
                 pltpu.SemaphoreType.REGULAR((down,)),
                 pltpu.SemaphoreType.REGULAR((down,)),

time: 9.45 us -> 9.3 us (0.984)
  Pallas kernels: 8.63 us -> 8.5 us
    pallas_call x1, Pallas kernels: 7.56 us -> 7.43 us  [local(): pl.pallas_call(functools.partial(exchange, across, down, sizes), out_shap...]
where the time goes in v6:
time: 9.3 us; the launch traced here: 9.14 us
  Pallas kernels  8.5 us (91%)
  between operations  0.64 us (7%)
    pallas_call x1, Pallas kernels, local(): pl.pallas_call(functools.partial(exchange, across, down, sizes), out_shap...  7.43 us
    pallas_call x1, Pallas kernels, local(): pl.pallas_call(functools.partial(compute, across, down, sizes), out_shape...  1.07 us

profile of v6, /device:TPU:1, one launch (start us, length us, event | category | flops | bytes accessed | tf_op | source)
XLA Modules:
  0.0 9.1 jit_solution(8341815736515171150)
XLA Ops:
  0.6 7.4 %shard_map.68 = (f32[3,4,16,256]{3,2,1,0:T(8,128)S(1)}, f32[3,8,256]{2,1,0:T(8,128)S(1)}, f32[216,256]{1,0:T(8,128)S(1)}, f32[2,216,256]{2,1,0:T(8,128)S(1)}, f3...) custom-call(f32[4,16,256]{2,1,0:T(8,128)} %potential.1, ...), custom_call_target="tpu_custom_call" | custom-call | tf_op jit(solution)/shard_map/pallas_call | solution.py:915
  8.1 1.1 %shard_map.69 = (f32[4,16,256]{2,1,0:T(8,128)}, f32[4,16,256]{2,1,0:T(8,128)}) custom-call(f32[3,4,16,256]{3,2,1,0:T(8,128)S(1)} %get-tuple-element.16.fibers, f32[3,8,256]{2,1,0:T(8,128)S(1)} %get-tuple-element.17.rim_fibers, f32[216,256]{1,0:T(8,128)S(1)} %get-tuple-element.18.refined, f32[2,216,256]{2,1,0:T(8,128)S(1)} %get-tuple-element.19.diffs, ...), custom_call_target="tpu_custom_call" | custom-call | tf_op jit(solution)/shard_map/pallas_call | solution.py:941

commit v7 on v6

--- a/solution.py
+++ b/solution.py
@@ -735,13 +735,13 @@
         slope.with_x(j)
 
     wait_plane_slots(slot_sem.at[0])
+    index_middle = gather_index(place, near_slots, 1, 0)
+    index_side = gather_index(place, near_slots, 1 - leave, -leave)
     if relayed:
         pl.when(jnp.logical_not(forwards))(lambda: drain_bytes((2 * down - 1) * table, near_sem.at[2]))
         pl.when(forwards)(lambda: drain_bytes((2 * down - 2) * table, near_sem.at[2]))
     else:
         drain_bytes((2 * down - 1) * table, near_sem.at[2])
-    index_middle = gather_index(place, near_slots, 1, 0)
-    index_side = gather_index(place, near_slots, 1 - leave, -leave)
     weight_y, weight_z = spread_y[...], spread_z[...]
     middle_row = pick_row(place, held, 1, index_middle)
     refined[...] = refine_row(place, middle_row, weight_y, weight_z, True)

time: 9.3 us -> 9.25 us (level)
  no operation moved by 1% of the time
where the time goes in v7:
time: 9.25 us; the launch traced here: 9.09 us
  Pallas kernels  8.45 us (91%)
  between operations  0.64 us (7%)
    pallas_call x1, Pallas kernels, local(): pl.pallas_call(functools.partial(exchange, across, down, sizes), out_shap...  7.38 us
    pallas_call x1, Pallas kernels, local(): pl.pallas_call(functools.partial(compute, across, down, sizes), out_shape...  1.07 us

profile of v7, /device:TPU:1, one launch (start us, length us, event | category | flops | bytes accessed | tf_op | source)
XLA Modules:
  0.0 9.1 jit_solution(6435266490425166591)
XLA Ops:
  0.6 7.4 %shard_map.68 = (f32[3,4,16,256]{3,2,1,0:T(8,128)S(1)}, f32[3,8,256]{2,1,0:T(8,128)S(1)}, f32[216,256]{1,0:T(8,128)S(1)}, f32[2,216,256]{2,1,0:T(8,128)S(1)}, f3...) custom-call(f32[4,16,256]{2,1,0:T(8,128)} %potential.1, ...), custom_call_target="tpu_custom_call" | custom-call | tf_op jit(solution)/shard_map/pallas_call | solution.py:915
  8.0 1.1 %shard_map.69 = (f32[4,16,256]{2,1,0:T(8,128)}, f32[4,16,256]{2,1,0:T(8,128)}) custom-call(f32[3,4,16,256]{3,2,1,0:T(8,128)S(1)} %get-tuple-element.16.fibers, f32[3,8,256]{2,1,0:T(8,128)S(1)} %get-tuple-element.17.rim_fibers, f32[216,256]{1,0:T(8,128)S(1)} %get-tuple-element.18.refined, f32[2,216,256]{2,1,0:T(8,128)S(1)} %get-tuple-element.19.diffs, ...), custom_call_target="tpu_custom_call" | custom-call | tf_op jit(solution)/shard_map/pallas_call | solution.py:941

commit v8 on v7

--- a/solution.py
+++ b/solution.py
@@ -353,7 +353,6 @@
     refined,
     diffs,
     volts,
-    slopes,
     parts_x,
     parts_y,
     parts_z,
@@ -361,7 +360,9 @@
     base,
     next_recovery,
     conducts,
+    late_fibers,
     cells,
+    slopes,
     held,
     near_slots,
     rest_in,
@@ -737,6 +738,18 @@
     wait_plane_slots(slot_sem.at[0])
     index_middle = gather_index(place, near_slots, 1, 0)
     index_side = gather_index(place, near_slots, 1 - leave, -leave)
+    edge = bx + 1
+
+    def late_local():
+        spot = place.slab(edge)
+        put_volts(place, cells, volts, slopes, spot, edge)
+        slope.along_x(bx)
+        slope.with_x(bx)
+        angles_there = [cells[number, spot, TOP : TOP + by] for number in (1, 2)]
+        for number, value in enumerate(fiber_of(*angles_there)):
+            late_fibers[number] = value
+
+    pl.when(jnp.logical_not(place.leaves))(late_local)
     if relayed:
         pl.when(jnp.logical_not(forwards))(lambda: drain_bytes((2 * down - 1) * table, near_sem.at[2]))
         pl.when(forwards)(lambda: drain_bytes((2 * down - 2) * table, near_sem.at[2]))
@@ -799,6 +812,7 @@
         row = [a - b for a, b in zip(row, (middle[0:8], middle[8:9]))]
         diffs[1] = refine_row(place, row, spread_y[...], spread_z[...], False)
         early_slab(0)
+        late_local()
 
 
 def compute(
@@ -810,7 +824,6 @@
     refined,
     diffs,
     volts,
-    slopes,
     parts_x,
     parts_y,
     parts_z,
@@ -818,7 +831,7 @@
     base,
     recovered,
     early_conducts,
-    cells,
+    late_fibers,
     next_potential,
     next_recovery,
     conducts,
@@ -832,10 +845,6 @@
     pltpu.make_async_copy(recovered, next_recovery, out_sem.at[0]).start()
 
     which = jnp.where(place.leaves, 1, 0)
-    put_volts(place, cells, volts, slopes, place.slab(bx + 1), bx + 1)
-    slope = Slopes(place, volts, slopes, parts_x, parts_y, parts_z)
-    slope.along_x(bx)
-    slope.with_x(bx)
 
     def finish(j):
         target = next_potential.at[place.slab(j) - 1]
@@ -853,8 +862,7 @@
         def fiber_at(rows, j=j, spot=spot):
             if j <= bx:
                 return [fibers[number, spot - 1, rows] for number in range(3)]
-            start = TOP + rows.start
-            return fiber_of(*(cells[number, spot, start : start + 8] for number in (1, 2)))
+            return [late_fibers[number, rows] for number in range(3)]
 
         def note(rows, excess, j=j, spot=spot):
             voltage = load_rows(volts, (j,), TOP + rows.start, 8)
@@ -902,7 +910,6 @@
             pltpu.VMEM((fine, nz), f32),
             pltpu.VMEM((2, fine, nz), f32),
             rows,
-            rows,
             pltpu.VMEM((bx + 1, 3, by, nz), f32),
             pltpu.VMEM((bx, 2, 3, by, nz), f32),
             pltpu.VMEM((bx, 3, by, nz), f32),
@@ -910,7 +917,7 @@
             pltpu.VMEM((bx, by, nz), f32),
             pltpu.VMEM((bx, by, nz), f32),
             pltpu.VMEM((6, half + 1, planes, by + 16, LANES), f32),
-            pltpu.VMEM((3, bx + 2, by + 16, nz), f32),
+            pltpu.VMEM((3, by, nz), f32),
         )
         arrived = pl.pallas_call(
             functools.partial(exchange, across, down, sizes),
@@ -918,6 +925,8 @@
             in_specs=[pl.BlockSpec(memory_space=pltpu.MemorySpace.HBM)] * 5,
             out_specs=(in_vmem,) * len(passed),
             scratch_shapes=[
+                pltpu.VMEM((3, bx + 2, by + 16, nz), f32),
+                rows,
                 pltpu.VMEM((3, down, 8 * blocks + 8, LANES), f32),
                 pltpu.VMEM((3, 3, ex, ey, ez), jnp.int32),
                 pltpu.VMEM(recovery.shape, f32),

time: 9.25 us -> 9.2 us (level)
  no operation moved by 1% of the time
where the time goes in v8:
time: 9.2 us; the launch traced here: 9.04 us
  Pallas kernels  8.4 us (91%)
  between operations  0.64 us (7%)
    pallas_call x1, Pallas kernels, local(): pl.pallas_call(functools.partial(exchange, across, down, sizes), out_shap...  7.39 us
    pallas_call x1, Pallas kernels, local(): pl.pallas_call(functools.partial(compute, across, down, sizes), out_shape...  1.01 us

profile of v8, /device:TPU:1, one launch (start us, length us, event | category | flops | bytes accessed | tf_op | source)
XLA Modules:
  0.0 9.0 jit_solution(12074891006407405509)
XLA Ops:
  0.6 7.4 %shard_map.68 = (f32[3,4,16,256]{3,2,1,0:T(8,128)S(1)}, f32[3,8,256]{2,1,0:T(8,128)S(1)}, f32[216,256]{1,0:T(8,128)S(1)}, f32[2,216,256]{2,1,0:T(8,128)S(1)}, f3...) custom-call(f32[4,16,256]{2,1,0:T(8,128)} %potential.1, ...), custom_call_target="tpu_custom_call" | custom-call | tf_op jit(solution)/shard_map/pallas_call | solution.py:922
  8.0 1.0 %shard_map.69 = (f32[4,16,256]{2,1,0:T(8,128)}, f32[4,16,256]{2,1,0:T(8,128)}) custom-call(f32[3,4,16,256]{3,2,1,0:T(8,128)S(1)} %get-tuple-element.15.fibers, f32[3,8,256]{2,1,0:T(8,128)S(1)} %get-tuple-element.16.rim_fibers, f32[216,256]{1,0:T(8,128)S(1)} %get-tuple-element.17.refined, f32[2,216,256]{2,1,0:T(8,128)S(1)} %get-tuple-element.18.diffs, ...), custom_call_target="tpu_custom_call" | custom-call | tf_op jit(solution)/shard_map/pallas_call | solution.py:950
